TPU v7x, 128 devices: a whole 4x4x4 slice. The times are simulated.
128 devices in a mesh: seq: 4 (over x_lo, core), tensor: 32 (over z, y, x_hi).
Axes of the slice: x: 4 (x_hi: 2, x_lo: 2; x = x_hi * 2 + x_lo), y: 4, z: 4, core: 2. Of those that a mesh axis runs over, the one named last changes fastest.
Arguments:
- tokens: bfloat16 [2, 4096, 4096], P(None, 'seq', 'tensor'), may hold values from -6 to 6
- w_qkv: bfloat16 [4096, 3, 4096], P(None, None, 'tensor'), may hold values from -1 to 1
- q_gain: float32 [4096], P('tensor'), may hold values from 0.5 to 2.5
- k_gain: float32 [4096], P('tensor'), may hold values from 0.5 to 2.5
- w_out: bfloat16 [4096, 4096], P('tensor'), may hold values from -0.1875 to 0.1875
Outputs:
- mixed: bfloat16 [2, 4096, 4096], P(None, 'seq', 'tensor')
- peak: float32 [32], P('tensor')
- qk_scale: float32 [2, 2, 4096], P(None, None, 'seq')
All inputs are finite; a program needn't handle non-finite values.
Results may differ from a plain program's by a relative error of at most 0.024.
Values may be sent and summed in bfloat16 or wider, within the bound.
A program may use at most 128 MiB of HBM per device.

v0:
```python
import jax
import jax.numpy as jnp
from jax import lax
from jax.sharding import Mesh
from jax.sharding import PartitionSpec as P

HEADS = 32
TENSOR = ("tensor_0", "tensor_1", "tensor_2")


EPS = 1e-06
ROPE_BASE = 500000.0
NEG = -1e30


def sent_to_all(array, axis):
    size = lax.axis_size(axis)
    return lax.all_to_all(
        jnp.broadcast_to(array[None], (size, *array.shape)), axis, 0, 0, tiled=True
    )


def taken_together(array, axis):
    return sent_to_all(array, axis).sum(axis=0)


def side_by_side(arrays, axis, dim, along):
    both = jnp.concatenate(arrays, axis=along)
    filled, at, gathered = (lax.all_gather(both, axis, axis=dim, tiled=True), 0, [])
    for a in arrays:
        gathered.append(lax.slice_in_dim(filled, at, at + a.shape[along], axis=along))
        at += a.shape[along]
    return tuple(gathered)


def over_copies(array, axis):
    return sent_to_all(array, axis).max(axis=0)


def sum_by_axis(array, axes, dim):
    for axis in axes:
        array = lax.psum_scatter(array, axis, scatter_dimension=dim, tiled=True)
    return array


def rope_tables(positions, head):
    half = head // 2
    freq = ROPE_BASE ** (-(jnp.arange(half, dtype=jnp.float32) * 2.0) / head)
    angle = positions[:, None] * freq[None, :]
    return (jnp.cos(angle), jnp.sin(angle))


def rotate(values, cosine, sine):
    half = values.shape[-1] // 2
    first = values[..., :half]
    second = values[..., half:]
    cosine = cosine[:, None, :]
    sine = sine[:, None, :]
    return jnp.concatenate([first * cosine - second * sine, second * cosine + first * sine], -1)


def norm_stats(query, keyed, width):
    totals = taken_together(
        jnp.stack([jnp.sum(query * query, 1), jnp.sum(keyed * keyed, 1)]), TENSOR
    )
    return lax.rsqrt(totals / width + EPS)


def online_update(q_part, k_part, v_part, valid, state, scale):
    top, denom, accum = state
    scores = jnp.einsum("sqd,skd->sqk", q_part, k_part, preferred_element_type=jnp.float32) * scale
    scores = jnp.where(valid[None], scores, NEG)
    new_top = jnp.maximum(top, jnp.max(scores, -1))
    weights = jnp.where(valid[None], jnp.exp(scores - new_top[..., None]), 0.0)
    factor = jnp.exp(top - new_top)
    added = jnp.einsum(
        "sqk,skd->sqd", weights.astype(jnp.bfloat16), v_part, preferred_element_type=jnp.float32
    )
    return (new_top, denom * factor + jnp.sum(weights, -1), accum * factor[..., None] + added)


def shards(tokens, w_qkv, q_gain, k_gain, w_out):
    seqs, tok, dloc = tokens.shape
    width = w_qkv.shape[0]
    head = width // HEADS
    heads_here = dloc // head
    rows = seqs * tok
    flat_w = w_qkv.reshape(width, 3 * dloc)
    whole = lax.all_gather(tokens, TENSOR, axis=2, tiled=True).reshape(rows, width)
    paired = jnp.dot(whole, flat_w[:, : 2 * dloc], preferred_element_type=jnp.float32)
    query = paired[:, :dloc]
    keyed = paired[:, dloc:]
    inverse = norm_stats(query, keyed, width)
    value = jnp.dot(whole, flat_w[:, 2 * dloc :], preferred_element_type=jnp.float32)
    own_index = lax.axis_index("seq")
    q_index = own_index * tok + jnp.arange(tok, dtype=jnp.int32)
    cosine, sine = rope_tables(q_index.astype(jnp.float32), head)

    def prepare(projection, scale_row, gain):
        normed = projection * scale_row[:, None] * gain[None, :]
        return rotate(normed.reshape(seqs, tok, heads_here, head), cosine, sine).astype(
            jnp.bfloat16
        )

    q_heads = prepare(query, inverse[0], q_gain).transpose(2, 0, 1, 3)
    k_ready = prepare(keyed, inverse[1], k_gain).reshape(seqs, tok, dloc)
    v_ready = value.astype(jnp.bfloat16).reshape(seqs, tok, dloc)
    scale = head ** (-0.5)
    keys_all, values_all = side_by_side((k_ready, v_ready), "seq", 1, 0)
    total_len = keys_all.shape[1]
    k_heads = keys_all.reshape(seqs, total_len, heads_here, head).transpose(2, 0, 1, 3)
    v_heads = values_all.reshape(seqs, total_len, heads_here, head).transpose(2, 0, 1, 3)

    def attend(operands):
        q_one, k_one, v_one = operands

        def visit(step, state):
            first = step * tok
            k_part = lax.dynamic_slice_in_dim(k_one, first, tok, 1)
            v_part = lax.dynamic_slice_in_dim(v_one, first, tok, 1)
            valid = (first + jnp.arange(tok, dtype=jnp.int32))[None, :] <= q_index[:, None]
            return online_update(q_one, k_part, v_part, valid, state, scale)

        initial = (
            jnp.full((seqs, tok), NEG, jnp.float32),
            jnp.zeros((seqs, tok), jnp.float32),
            jnp.zeros((seqs, tok, head), jnp.float32),
        )
        top, denom, accum = lax.fori_loop(0, own_index + 1, visit, initial)
        return (accum / denom[..., None], top)

    outputs, tops = lax.map(attend, (q_heads, k_heads, v_heads))
    attended = outputs.astype(jnp.bfloat16).transpose(1, 2, 0, 3).reshape(rows, dloc)
    peak = over_copies(jnp.max(tops, axis=(1, 2)), "seq")
    partial_out = (
        jnp.dot(attended, w_out, preferred_element_type=jnp.float32)
        .astype(jnp.bfloat16)
        .reshape(seqs, tok, width)
    )
    mixed = sum_by_axis(partial_out, TENSOR, 2).astype(jnp.float32)
    return (mixed.astype(jnp.bfloat16), peak, inverse.reshape(2, seqs, tok))


def solution(mesh):
    finer = Mesh(
        mesh.devices.reshape(mesh.shape["seq"], 4, 4, 2),
        ("seq", "tensor_0", "tensor_1", "tensor_2"),
    )
    placed = (P(None, "seq", TENSOR), P(None, None, TENSOR), P(TENSOR), P(TENSOR), P(TENSOR, None))
    return jax.shard_map(
        shards,
        mesh=finer,
        in_specs=placed,
        out_specs=(P(None, "seq", TENSOR), P(TENSOR), P(None, None, "seq")),
        check_vma=False,
    )
```

profile of v0, /device:TPU:1, one launch (start us, length us, event | category | flops | bytes accessed | tf_op | source)
XLA Modules:
  0.0 593.4 jit_solution(10021887254225840839)
XLA Ops:
  7.2 0.0 copy-start
  7.2 0.0 all-gather.3.cloned.1.call-start
  7.2 0.7 all-gather.3.cloned.1.call-update
  7.9 4.7 copy.16
  12.7 3.1 multiply_cosine_fusion
  15.7 205.0 %all-gather.3.cloned.1.call-done = bf16[2,1024,4096]{2,1,0:T(8,128)(2,1)} async-done(((bf16[2,1024,128]{2,1,0:T(8,128)(2,1)}), bf16[2,1024,4096]{2,1,0:T(8,128)(2,1)}) %all-gather.3.cloned.1.call-update) | async-done | bytes 16777232 | tf_op jit(solution)/shard_map/all_gather | solution.py:89
  220.7 8.8 %fusion.19 = f32[2048,256]{1,0:T(8,128)S(1)} fusion(bf16[2048,4096]{1,0:T(8,128)(2,1)} %bitcast.64, bf16[4096,384]{0,1:T(8,128)(2,1)} %bitcast.55), kind=kOutput, calls=%fused_computation.24 | convolution fusion | flops 4294967296 | bytes 20971520 | tf_op jit(solution)/shard_map/dot_general | solution.py:90
  229.5 0.6 multiply_reduce_fusion.1
  230.1 1.0 broadcast_in_dim.36
  231.2 5.4 all-to-all-start
  236.6 0.0 copy-start.2
  236.6 0.0 copy-start.3
  236.6 0.0 all-gather.5.cloned.1.call-start
  236.7 11.3 %convolution_convert_fusion.1 = bf16[2048,128]{1,0:T(8,128)(2,1)} fusion(bf16[2048,4096]{1,0:T(8,128)(2,1)} %bitcast.65, bf16[4096,384]{0,1:T(8,128)(2,1)} %bitcast.56), kind=kOutput, calls=%fused_computation.23 | convolution fusion | flops 2147745792 | bytes 18350080 | tf_op jit(solution)/shard_map/dot_general | solution.py:94
  248.0 0.5 all-to-all-done
  248.5 1.2 reduce_sum.38
  249.8 0.0 copy-start.1
  249.8 0.0 copy-done.2
  249.8 0.0 copy-done.3
  249.8 0.7 multiply_multiply_fusion
  250.6 2.0 fusion.24
  252.5 0.0 copy-done.1
  252.5 1.3 pad_maximum_fusion
  253.8 0.0 all-gather.5.cloned.1.call-update
  253.8 0.2 reduce-scatter.6.cloned.1.call-start
  254.1 1.1 pad_maximum_fusion.1
  255.1 48.1 %all-gather.5.cloned.1.call-done = bf16[4,4096,128]{2,1,0:T(8,128)(2,1)} async-done(((bf16[4,1024,128]{2,1,0:T(8,128)(2,1)}), bf16[4,4096,128]{2,1,0:T(8,128)(2,1)}) %all-gather.5.cloned.1.call-update) | async-done | bytes 4194320 | tf_op jit(solution)/shard_map/all_gather | solution.py:29
  303.3 4.5 fusion.26
  307.7 0.1 broadcast.114
  307.8 21.6 %while.25 = (s32[]{:T(128)}, f32[2,1024]{1,0:T(2,128)S(1)}, f32[2,1024]{1,0:T(2,128)S(1)}, f32[2,1024,128]{2,1,0:T(8,128)S(1)}, s32[]{:T(128)}, /*index=5*/bf16[...) while((s32[]{:T(128)}, f32[2,1024]{1,0:T(2,128)S(1)}, ...), condition=%wide.region_6.7_spmd.clone, body=%wide.region_3.6_spmd.clone.sunk | while | flops 1102583808 | bytes 33177796 | solution.py:129
  307.8 0.7 broadcast_compare_fusion.2
  308.5 3.0 fusion.42
  311.5 2.3 fusion.43
  313.8 4.8 fusion.44
  318.6 0.7 broadcast_compare_fusion.2
  319.3 3.0 fusion.42
  322.3 2.3 fusion.43
  324.6 4.8 fusion.44
  329.4 0.3 divide_convert_fusion
  329.7 0.0 copy-done
  329.7 8.0 %convolution_convert_fusion = bf16[2048,4096]{1,0:T(8,128)(2,1)} fusion(bf16[2048,128]{1,0:T(8,128)(2,1)S(1)} %bitcast.57, bf16[128,4096]{1,0:T(8,128)(2,1)S(1)} %copy-done), kind=kOutput, calls=%fused_computation.22 | convolution fusion | flops 2155872256 | bytes 18350080 | tf_op jit(solution)/shard_map/dot_general | solution.py:136
  337.8 0.0 reduce-scatter.6.cloned.1.call-update
  337.8 0.0 reduce-scatter.8.cloned.1.call-start
  337.9 169.6 %reduce-scatter.6.cloned.1.call-done = bf16[2,1024,1024]{2,1,0:T(8,128)(2,1)} async-done(((bf16[2,1024,4096]{2,1,0:T(8,128)(2,1)}), bf16[2,1024,1024]{2,1,0:T(8,128)(2,1)}) %reduce-scatter.6.cloned.1.call-update) | async-done | bytes 4194320 | tf_op jit(solution)/shard_map/reduce_scatter | solution.py:42
  507.5 0.0 reduce-scatter.8.cloned.1.call-update
  507.5 0.0 reduce-scatter.10.cloned.1.call-start
  507.6 48.6 %reduce-scatter.8.cloned.1.call-done = bf16[2,1024,256]{2,1,0:T(8,128)(2,1)} async-done(((bf16[2,1024,1024]{2,1,0:T(8,128)(2,1)}), bf16[2,1024,256]{2,1,0:T(8,128)(2,1)}) %reduce-scatter.8.cloned.1.call-update) | async-done | bytes 1048592 | tf_op jit(solution)/shard_map/reduce_scatter | solution.py:42
  556.2 2.6 copy.20
  558.8 1.3 copy.24
  560.0 0.0 reduce-scatter.10.cloned.1.call-update
  560.1 0.6 rsqrt.8
  560.7 0.6 reduce_max.29
  561.3 0.6 broadcast_in_dim.37
  562.0 6.4 %all_to_all.11 = f32[4,1,1]{2,1,0:T(1,128)S(1)} all-to-all(f32[4,1,1]{2,1,0:T(1,128)S(1)} %broadcast_in_dim.37), channel_id=1, replica_groups=mesh['seq'=4,'tensor_0'=4,'tensor_1'=4,'tensor_2'=2] {'seq'}, dimensions={0} | all-to-all | bytes 32 | tf_op jit(solution)/shard_map/all_to_all | solution.py:18
  568.3 0.6 reduce_max.30
  568.9 15.3 %reduce-scatter.10.cloned.1.call-done = bf16[128,2048]{1,0:T(8,128)(2,1)} async-done(((bf16[256,2048]{1,0:T(8,128)(2,1)}), bf16[128,2048]{1,0:T(8,128)(2,1)}) %reduce-scatter.10.cloned.1.call-update) | async-done | bytes 524304
  584.2 1.4 reshape.187
  585.7 1.2 copy.21
  (15 shorter events, 0.1 us)
Async XLA Ops:
  7.2 322.6 %copy-start = (bf16[128,4096]{1,0:T(8,128)(2,1)S(1)}, bf16[128,4096]{1,0:T(8,128)(2,1)}, u32[]{:S(2)}) copy-start(bf16[128,4096]{1,0:T(8,128)(2,1)} %param.11) | copy-start | bytes 3145732
  7.2 213.6 %all-gather.3.cloned.1.call-start = ((), (), s32[]{:S(2)}) async-start(), calls=%async_computation.5 | async-start | bytes 17301504 | tf_op jit(solution)/shard_map/all_gather | solution.py:89
  231.2 17.4 %all-to-all-start = ((f32[32,2,2048]{2,1,0:T(2,128)}), f32[32,2,2048]{2,1,0:T(2,128)}, u32[]{:S(2)}, u32[]{:S(2)}) async-start(f32[32,2,2048]{2,1,0:T(2,128)} %broadcast_in_dim.36), calls=%async_computation | async-start | bytes 1048576 | tf_op jit(solution)/shard_map/all_to_all | solution.py:18
  236.6 13.2 %copy-start.2 = (f32[128]{0:T(128)S(1)}, f32[128]{0:T(128)}, u32[]{:S(2)}) copy-start(f32[128]{0:T(128)} %param.9) | copy-start | bytes 1540
  236.6 13.2 %copy-start.3 = (f32[128]{0:T(128)S(1)}, f32[128]{0:T(128)}, u32[]{:S(2)}) copy-start(f32[128]{0:T(128)} %param.10) | copy-start | bytes 1540
  236.6 66.6 %all-gather.5.cloned.1.call-start = ((), (), s32[]{:S(2)}) async-start(), calls=%async_computation.6 | async-start | bytes 5242880 | tf_op jit(solution)/shard_map/all_gather | solution.py:29
  249.8 2.8 copy-start.1
  253.8 253.7 %reduce-scatter.6.cloned.1.call-start = ((), (), s32[]{:S(2)}) async-start(), calls=%async_computation.7 | async-start | bytes 20971520 | tf_op jit(solution)/shard_map/reduce_scatter | solution.py:42
  337.8 218.4 %reduce-scatter.8.cloned.1.call-start = ((), (), s32[]{:S(2)}) async-start(), calls=%async_computation.8 | async-start | bytes 5242880 | tf_op jit(solution)/shard_map/reduce_scatter | solution.py:42
  507.5 76.7 %reduce-scatter.10.cloned.1.call-start = ((), (), s32[]{:S(2)}) async-start(), calls=%async_computation.9 | async-start | bytes 1572864
Sparse Core Ops, SparseCore 0:
  10.7 209.9 all-gather.2
  253.9 49.2 all-gather.4
  337.9 169.4 reduce-scatter.5
  509.7 46.4 reduce-scatter.7
  560.2 24.0 reduce-scatter.9
where the time goes:
time: 594 us; the launch traced here: 593 us
  waiting for transfers between devices  488 us (82%)
  matrix products  43.7 us (7%)
  local copies, waits for them, and re-layouts  18.1 us (3%)
  other arithmetic  17.4 us (3%)
  between operations  14 us (2%)
  blocking collectives  6.36 us (1%)
    reduce_scatter x2, waiting for transfers between devices, sum_by_axis(): array = lax.psum_scatter(array, axis, scatter_dimension=dim, tiled=True)  218 us
    all_gather x1, waiting for transfers between devices, shards(): lax.all_gather(tokens, TENSOR, axis=2, tiled=True).reshape(rows, width)  205 us
    all_gather x1, waiting for transfers between devices, side_by_side(): lax.all_gather(both, axis, axis=dim, tiled=True)  48.1 us
    unnamed x6, waiting for transfers between devices  16.1 us
  transfers between devices with their start and end apart: 6, of which 6 were waited for; matrix products, arithmetic and copies ran while one was open for 4% of the time, Pallas kernels for 0%

commit v1 on v0

v1 whole, which is shorter than its diff:
```python
import functools

import jax
import jax.numpy as jnp
from jax import lax
from jax.experimental import pallas as pl
from jax.experimental.pallas import tpu as pltpu
from jax.sharding import Mesh
from jax.sharding import PartitionSpec as P

EPS = 1e-06
ROPE_BASE = 500000.0
NEG = -1e30
MESH = pl.DeviceIdType.MESH
HEAD = 128
TOK = 1024
HALF = TOK // 2
WIDTH = 4096
VMEM_CAP = 60 * 1024 * 1024
COPIES = 40


def here():
    xh, xl = lax.axis_index("xh"), lax.axis_index("xl")
    return xh * 2 + xl, xh, xl, lax.axis_index("co"), lax.axis_index("z"), lax.axis_index("y")


def seq_of(x):
    return 1 - ((x + 1) // 2) % 2


def half_of(x):
    return 1 - x % 2


def at_x(x, core=None):
    dev = {"xl": x % 2, "xh": x // 2}
    if core is not None:
        dev["co"] = core
    return dev


def greet(devices):
    barrier = pltpu.get_barrier_semaphore()
    for dev in devices:
        pl.semaphore_signal(barrier, inc=1, device_id=dev, device_id_type=MESH)
    pl.semaphore_wait(barrier, len(devices))


def remote(src, dst, ssem, rsem, dev):
    return pltpu.make_async_remote_copy(
        src_ref=src, dst_ref=dst, send_sem=ssem, recv_sem=rsem, device_id=dev, device_id_type=MESH
    )


def gather(buf, ssem, rsem, z, y, own_ready, use):
    sent = []
    count = [0]

    def place(h, f, s):
        return (f % 4, s % 4) if h == 0 else (s % 4, f % 4)

    first = (z, y)
    second = (y, z)
    axis = (("z", "y"), ("y", "z"))

    def send(h, f, s, part, along, dirn):
        zz, yy = place(h, f, s)
        ref = buf.at[h, zz, yy] if part is None else buf.at[h, zz, yy, part]
        name = axis[h][along]
        me = (first[h], second[h])[along]
        c = count[0]
        count[0] += 1
        cp = remote(ref, ref, ssem.at[c], rsem.at[c], {name: (me + dirn + 4) % 4})
        cp.start()
        sent.append(cp)
        return cp

    p1, p1f, p2, p2f = {}, {}, {}, {}
    part_of = {1: 0, -1: 1}
    dirs = (1, -1)
    for h in (0, 1):
        own_ready(h)
        f, s = first[h], second[h]
        for d in dirs:
            p1[h, d] = send(h, f, s, None, 0, d)
        if h == 1:
            for g in (0, 1):
                for d in dirs:
                    p2[g, 0, d] = send(g, first[g], second[g], None, 1, d)
    for h in (0, 1):
        use(h, *place(h, first[h], second[h]))
    for d in dirs:
        for h in (0, 1):
            f, s = first[h], second[h]
            p1[h, d].wait_recv()
            p1f[h, d] = send(h, f - d + 4, s, part_of[d], 0, d)
            for e in dirs:
                p2[h, -d, e] = send(h, f - d + 4, s, None, 1, e)
    for d in dirs:
        for h in (0, 1):
            use(h, *place(h, first[h] - d + 4, second[h]))
    for d in dirs:
        for h in (0, 1):
            p2[h, 0, d].wait_recv()
            p2f[h, 0, d] = send(h, first[h], second[h] - d + 4, part_of[d], 1, d)
    for h in (0, 1):
        for d in dirs:
            p1f[h, d].wait_recv()
        for d in dirs:
            p2[h, 2, d] = send(h, first[h] + 2, second[h], None, 1, d)
    for h in (0, 1):
        for d in dirs:
            use(h, *place(h, first[h], second[h] - d + 4))
        use(h, *place(h, first[h] + 2, second[h]))
    for j in (-1, 1, 2):
        for h in (0, 1):
            f, s = first[h], second[h]
            for d in dirs:
                p2[h, j, d].wait_recv()
                p2f[h, j, d] = send(h, f + j + 4, s - d + 4, part_of[d], 1, d)
        for h in (0, 1):
            for d in dirs:
                use(h, *place(h, first[h] + j + 4, second[h] - d + 4))
    for j in (0, -1, 1, 2):
        for h in (0, 1):
            for d in dirs:
                p2f[h, j, d].wait_recv()
            use(h, *place(h, first[h] + j + 4, second[h] + 2))
    return sent


def block_dot(acc, buf, w, h, zz, yy):
    base = pl.multiple_of((zz * 4 + yy) * 256, 256)
    rhs = w[pl.ds(base, 256), :]
    lhs = jnp.concatenate([buf[h, zz, yy, 0], buf[h, zz, yy, 1]], axis=-1)
    rows = pl.ds(h * HALF, HALF)
    acc[rows, :] += jnp.dot(lhs, rhs, preferred_element_type=jnp.float32)


def qkv_kernel(
    tok, w_own, gains, cosf, sinf,
    q_out, k_out, v_out, stat_out,
    buf, w_far, gains_far, acc, acc_far, qx, kx, vx, zb, yb, inv, inv_in,
    ssem, rsem, xs, xr,
):
    x, xh, xl, co, z, y = here()
    right, left, pair = (x + 1) % 4, (x + 3) % 4, 3 - x
    greet(
        [at_x(right), at_x(left), {"co": 1 - co}, at_x(pair, 1 - co)]
        + [{"z": (z + i) % 4} for i in (1, 2, 3)]
        + [{"y": (y + i) % 4} for i in (1, 2, 3)]
    )
    n = [0]
    sent = []

    def send(src, dst, dev):
        c = n[0]
        n[0] += 1
        cp = remote(src, dst, xs.at[c], xr.at[c], dev)
        cp.start()
        sent.append(cp)
        return cp

    toks = {}
    for h in (0, 1):
        rows = pl.ds(h * HALF, HALF)
        toks[h] = (
            send(tok.at[xh, rows], buf.at[h, z, y, xh], at_x(right)),
            send(tok.at[1 - xh, rows], buf.at[h, z, y, xh], at_x(left)),
        )
    far_g = send(gains, gains_far, at_x(pair))
    far_w = []
    for i in (0, 1):
        rows = pl.ds(pl.multiple_of((co * 2 + i) * 1024, 1024), 1024)
        far_w.append(send(w_own.at[rows], w_far.at[rows], at_x(pair)))
    acc[...] = jnp.zeros_like(acc)
    acc_far[...] = jnp.zeros_like(acc_far)

    def own_ready(h):
        for cp in toks[h]:
            cp.wait_recv()

    late = []
    relayed = []

    def use(h, zz, yy):
        block_dot(acc, buf, w_own, h, zz, yy)
        late.append((h, zz, yy))
        if len(late) == 20:
            for i in (0, 1):
                far_w[i].wait_recv()
                rows = pl.ds(pl.multiple_of((co * 2 + i) * 1024, 1024), 1024)
                relayed.append(send(w_far.at[rows], w_far.at[rows], {"co": 1 - co}))
        if len(late) == 24:
            for cp in relayed:
                cp.wait_recv()
            for b in late:
                block_dot(acc_far, buf, w_far, *b)
        if len(late) > 24:
            block_dot(acc_far, buf, w_far, h, zz, yy)

    sent += gather(buf, ssem, rsem, z, y, own_ready, use)

    step = 256

    def squares(i, carry):
        rows = pl.ds(pl.multiple_of(i * step, step), step)
        for j in (0, 1):
            cols = pl.ds(j * HEAD, HEAD)
            a, b = acc[rows, cols], acc_far[rows, cols]
            zb[z, pl.ds(j, 1), rows] = jnp.sum((a * a + b * b).T, axis=0, keepdims=True)
        return carry

    lax.fori_loop(0, TOK // step, squares, 0)
    got = [send(zb.at[z], zb.at[z], {"z": (z + i) % 4}) for i in (1, 2, 3)]
    for cp in got:
        cp.wait_recv()
    yb[y] = (zb[0] + zb[1]) + (zb[2] + zb[3])
    got = [send(yb.at[y], yb.at[y], {"y": (y + i) % 4}) for i in (1, 2, 3)]
    for cp in got:
        cp.wait_recv()
    inv[...] = lax.rsqrt(((yb[0] + yb[1]) + (yb[2] + yb[3])) / WIDTH + EPS)
    me_seq = seq_of(x)
    stats = [send(inv, inv_in.at[me_seq], at_x(right)), send(inv, inv_in.at[me_seq], at_x(left))]
    far_g.wait_recv()

    mine = half_of(x) * 2 + co

    def rows_of(i, carry):
        rows = pl.ds(pl.multiple_of(i * step, step), step)
        cs, sn = cosf[rows, :], sinf[rows, :]

        def turned(a, j, g):
            col = jnp.broadcast_to(inv[pl.ds(j, 1), rows], (HEAD, step)).T
            t = a[rows, pl.ds(j * HEAD, HEAD)] * col * g[pl.ds(j, 1), :]
            return (t * cs + pltpu.roll(t, HEAD // 2, 1) * sn).astype(jnp.bfloat16)

        qx[rows, :] = turned(acc_far, 0, gains_far)
        kx[rows, :] = turned(acc_far, 1, gains_far)
        vx[rows, :] = acc_far[rows, pl.ds(2 * HEAD, HEAD)].astype(jnp.bfloat16)
        q_out[0, rows, :] = turned(acc, 0, gains)
        k_out[mine, rows, :] = turned(acc, 1, gains)
        v_out[mine, rows, :] = acc[rows, pl.ds(2 * HEAD, HEAD)].astype(jnp.bfloat16)
        return carry

    lax.fori_loop(0, TOK // step, rows_of, 0)
    other = {"co": 1 - co}
    far_q = send(qx, q_out.at[1], at_x(pair, 1 - co))
    far_k = send(kx, k_out.at[mine], at_x(pair))
    far_v = send(vx, v_out.at[mine], at_x(pair))
    near = [
        send(k_out.at[mine], k_out.at[mine], other),
        send(v_out.at[mine], v_out.at[mine], other),
    ]
    theirs = (1 - half_of(x)) * 2 + co
    far_k.wait_recv()
    near.append(send(k_out.at[theirs], k_out.at[theirs], other))
    far_v.wait_recv()
    near.append(send(v_out.at[theirs], v_out.at[theirs], other))
    for cp in stats:
        cp.wait_recv()
    for s in (0, 1):
        stat_out[:, s, :] = inv_in[s]
    far_q.wait_recv()
    for cp in near:
        cp.wait_recv()
    for cp in sent:
        cp.wait_send()


def attend_kernel(q, k, v, o, top_out):
    x, xh, xl, co, z, y = here()
    own = half_of(x) * 2 + co
    factor = (HEAD ** (-0.5)) * 1.4426950408889634
    bq, bk = 256, 512
    best = jnp.full((8, 128), NEG, jnp.float32)
    for which in (0, 1):
        quarter = own if which == 0 else (1 - half_of(x)) * 2 + (1 - co)

        def tile(i, best):
            rows = pl.ds(pl.multiple_of(i * bq, bq), bq)
            qt = q[which, rows, :]
            first = quarter * TOK + i * bq

            def visit(j, state, masked):
                top, den, out = state
                at = pl.multiple_of(j * bk, bk)
                keys = pl.ds(at, bk)
                s = lax.dot_general(
                    qt, k[keys, :], (((1,), (1,)), ((), ())), preferred_element_type=jnp.float32
                )
                if masked:
                    r = lax.broadcasted_iota(jnp.int32, (bq, bk), 0) + first
                    c = lax.broadcasted_iota(jnp.int32, (bq, bk), 1) + at
                    s = jnp.where(c <= r, s, NEG)
                new = jnp.maximum(top, jnp.max(s, axis=1, keepdims=True))
                e = jnp.exp2((s - new) * factor)
                keep = jnp.exp2((top - new) * factor)
                den = den * keep + jnp.sum(e, axis=1, keepdims=True)
                out = out * keep + jnp.dot(
                    e.astype(jnp.bfloat16), v[keys, :], preferred_element_type=jnp.float32
                )
                return new, den, out

            state = (
                jnp.full((bq, 1), NEG, jnp.float32),
                jnp.zeros((bq, 1), jnp.float32),
                jnp.zeros((bq, HEAD), jnp.float32),
            )
            last = first // bk
            state = lax.fori_loop(0, last, lambda j, st: visit(j, st, False), state)
            top, den, out = visit(last, state, True)
            o[which, rows, :] = (out / den).astype(jnp.bfloat16)
            return jnp.maximum(best, jnp.max(top))

        best = lax.fori_loop(0, TOK // bq, tile, best)
    top_out[...] = best * (HEAD ** (-0.5))


def mix_kernel(
    o, top, w,
    mixed, peak,
    buf, acc, ob, tops,
    ssem, rsem, xs, xr,
):
    x, xh, xl, co, z, y = here()
    right, left, pair = (x + 1) % 4, (x + 3) % 4, 3 - x
    same = xh * 2 + (1 - xl)
    greet(
        [at_x(right), at_x(left), {"co": 1 - co}, at_x(right, 1 - co), at_x(left, 1 - co)]
        + [{"z": (z + 1) % 4}, {"z": (z + 3) % 4}, {"y": (y + 1) % 4}, {"y": (y + 3) % 4}]
    )
    n = [0]
    sent = []

    def send(src, dst, dev):
        c = n[0]
        n[0] += 1
        cp = remote(src, dst, xs.at[c], xr.at[c], dev)
        cp.start()
        sent.append(cp)
        return cp

    back = {
        h: send(o.at[1, pl.ds(h * HALF, HALF)], buf.at[h, z, y, xh], at_x(pair, 1 - co))
        for h in (0, 1)
    }
    for h in (0, 1):
        buf[h, z, y, xh] = o[0, pl.ds(h * HALF, HALF), :]
    place = xl * 2 + co
    tops[place] = top[...]
    peaks = [
        send(tops.at[place], tops.at[place], dev)
        for dev in ({"co": 1 - co}, at_x(same), at_x(same, 1 - co))
    ]
    acc[...] = jnp.zeros_like(acc)

    def use(h, zz, yy):
        block_dot(acc, buf, w, h, zz, yy)

    sent += gather(buf, ssem, rsem, z, y, lambda h: back[h].wait_recv(), use)
    ob[0] = acc[:, 0:HEAD].astype(jnp.bfloat16)
    ob[1] = acc[:, HEAD:].astype(jnp.bfloat16)
    me_seq = seq_of(x)
    fin = [
        send(ob.at[right // 2], mixed.at[me_seq], at_x(right)),
        send(ob.at[left // 2], mixed.at[me_seq], at_x(left)),
    ]
    for cp in peaks:
        cp.wait_recv()
    peak[...] = jnp.maximum(jnp.maximum(tops[0], tops[1]), jnp.maximum(tops[2], tops[3]))
    for cp in fin:
        cp.wait_recv()
    for cp in sent:
        cp.wait_send()


def vmem(count):
    return [pl.BlockSpec(memory_space=pltpu.VMEM)] * count


def shards(tokens, w_qkv, q_gain, k_gain, w_out):
    x = lax.axis_index("xh") * 2 + lax.axis_index("xl")
    quarter = half_of(x) * 2 + lax.axis_index("co")
    w_own = w_qkv.reshape(WIDTH, 3 * HEAD)
    gains = jnp.concatenate([q_gain[None], k_gain[None], jnp.zeros((6, HEAD), jnp.float32)])
    positions = (quarter * TOK + jnp.arange(TOK, dtype=jnp.int32)).astype(jnp.float32)
    freq = ROPE_BASE ** (-(jnp.arange(HEAD // 2, dtype=jnp.float32) * 2.0) / HEAD)
    angle = positions[:, None] * freq[None, :]
    cosine, sine = jnp.cos(angle), jnp.sin(angle)
    cosf = jnp.concatenate([cosine, cosine], -1)
    sinf = jnp.concatenate([-sine, sine], -1)

    half_rows = lax.all_to_all(
        w_out.reshape(HEAD, 16, 256).transpose(1, 0, 2), ("z", "y"), 0, 0, tiled=True
    )
    both = lax.all_gather(half_rows, "xh", axis=1)
    w_cols = both.reshape(WIDTH, 256)

    bf, f32 = jnp.bfloat16, jnp.float32
    dma = pltpu.SemaphoreType.DMA
    q, k, v, stat = pl.pallas_call(
        qkv_kernel,
        out_shape=(
            jax.ShapeDtypeStruct((2, TOK, HEAD), bf),
            jax.ShapeDtypeStruct((4, TOK, HEAD), bf),
            jax.ShapeDtypeStruct((4, TOK, HEAD), bf),
            jax.ShapeDtypeStruct((2, 2, TOK), f32),
        ),
        in_specs=vmem(5),
        out_specs=tuple(vmem(4)),
        scratch_shapes=[
            pltpu.VMEM((2, 4, 4, 2, HALF, HEAD), bf),
            pltpu.VMEM((WIDTH, 3 * HEAD), bf),
            pltpu.VMEM((8, HEAD), f32),
            pltpu.VMEM((TOK, 3 * HEAD), f32),
            pltpu.VMEM((TOK, 3 * HEAD), f32),
            pltpu.VMEM((TOK, HEAD), bf),
            pltpu.VMEM((TOK, HEAD), bf),
            pltpu.VMEM((TOK, HEAD), bf),
            pltpu.VMEM((4, 2, TOK), f32),
            pltpu.VMEM((4, 2, TOK), f32),
            pltpu.VMEM((2, TOK), f32),
            pltpu.VMEM((2, 2, TOK), f32),
            dma((COPIES,)),
            dma((COPIES,)),
            dma((32,)),
            dma((32,)),
        ],
        compiler_params=pltpu.CompilerParams(
            collective_id=0, has_side_effects=True, vmem_limit_bytes=VMEM_CAP
        ),
        name="qkv",
    )(tokens, w_own, gains, cosf, sinf)

    o, top = pl.pallas_call(
        attend_kernel,
        out_shape=(
            jax.ShapeDtypeStruct((2, TOK, HEAD), bf),
            jax.ShapeDtypeStruct((8, HEAD), f32),
        ),
        in_specs=vmem(3),
        out_specs=tuple(vmem(2)),
        compiler_params=pltpu.CompilerParams(vmem_limit_bytes=VMEM_CAP),
        name="attend",
    )(q, k.reshape(4 * TOK, HEAD), v.reshape(4 * TOK, HEAD))

    mixed, peak = pl.pallas_call(
        mix_kernel,
        out_shape=(
            jax.ShapeDtypeStruct((2, TOK, HEAD), bf),
            jax.ShapeDtypeStruct((8, HEAD), f32),
        ),
        in_specs=vmem(3),
        out_specs=tuple(vmem(2)),
        scratch_shapes=[
            pltpu.VMEM((2, 4, 4, 2, HALF, HEAD), bf),
            pltpu.VMEM((TOK, 256), f32),
            pltpu.VMEM((2, TOK, HEAD), bf),
            pltpu.VMEM((4, 8, HEAD), f32),
            dma((COPIES,)),
            dma((COPIES,)),
            dma((8,)),
            dma((8,)),
        ],
        compiler_params=pltpu.CompilerParams(
            collective_id=1, has_side_effects=True, vmem_limit_bytes=VMEM_CAP
        ),
        name="mix",
    )(o, top, w_cols)
    return mixed, peak[0, :1], stat


def solution(mesh):
    finer = Mesh(mesh.devices.reshape(2, 2, 4, 4, 2), ("xl", "co", "z", "y", "xh"))
    tensor = ("z", "y", "xh")
    seq = ("xl", "co")
    placed = (P(None, seq, tensor), P(None, None, tensor), P(tensor), P(tensor), P(tensor, None))
    return jax.shard_map(
        shards,
        mesh=finer,
        in_specs=placed,
        out_specs=(P(None, seq, tensor), P(tensor), P(None, None, seq)),
        check_vma=False,
    )
```

time: 594 us -> 248 us (0.42)
  waiting for transfers between devices: 488 us -> 0.02 us
  Pallas kernels: 0 us -> 194 us
  matrix products: 43.7 us -> 0 us
  blocking collectives: 6.36 us -> 24.5 us
  other arithmetic: 17.4 us -> 3.94 us
  local copies, waits for them, and re-layouts: 18.1 us -> 11.1 us
    all_gather x2 -> x1, waiting for transfers between devices: 253 us -> 0.01 us  [shards(): both = lax.all_gather(half_rows, 'xh', axis=1)]
    reduce_scatter x2 -> x0, waiting for transfers between devices: 218 us -> none  [sum_by_axis(): array = lax.psum_scatter(array, axis, scatter_dimension=dim, tiled=True)]
    pallas_call x0 -> x3, Pallas kernels: none -> 194 us  [the longest x1 108 us: shards(): pl.pallas_call(qkv_kernel, out_shape=(jax.ShapeDtypeStruct((2, TOK, HEAD)...]
    dot_general x7 -> x0, matrix products: 43.7 us -> none  [the longest x1 11.3 us: shards(): jnp.dot(whole, flat_w[:, 2 * dloc:], preferred_element_type=jnp.float32)]
    all_to_all x1, blocking collectives: 6.36 us -> 24.5 us  [shards(): lax.all_to_all(w_out.reshape(HEAD, 16, 256).transpose(1, 0, 2), ('z', 'y'...]
    unnamed x6 -> x1, waiting for transfers between devices: 16.1 us -> 0.02 us
    reduce_sum x4 -> x0, other arithmetic: 6.33 us -> none  [the longest x2 4.51 us: online_update(): jnp.sum(weights, -1)]
  transfers between devices with their start and end apart: 6 -> 1, of which waited for: 6 -> 0; matrix products, arithmetic and copies ran while one was open for 4% -> 4% of each run, Pallas kernels for 0% -> 52%
where the time goes in v1:
time: 248 us
  Pallas kernels  194 us (78%)
  blocking collectives  24.5 us (10%)
  between operations  14.1 us (6%)
  local copies, waits for them, and re-layouts  11.1 us (4%)
  other arithmetic  3.94 us (2%)
    pallas_call x1, Pallas kernels, shards(): pl.pallas_call(qkv_kernel, out_shape=(jax.ShapeDtypeStruct((2, TOK, HEAD)...  108 us
    pallas_call x1, Pallas kernels, shards(): pl.pallas_call(mix_kernel, out_shape=(jax.ShapeDtypeStruct((2, TOK, HEAD)...  65.9 us
    all_to_all x1, blocking collectives, shards(): lax.all_to_all(w_out.reshape(HEAD, 16, 256).transpose(1, 0, 2), ('z', 'y'...  24.5 us
    pallas_call x1, Pallas kernels, shards(): pl.pallas_call(attend_kernel, out_shape=(jax.ShapeDtypeStruct((2, TOK, HE...  20.3 us
    unnamed x9, local copies, waits for them, and re-layouts  5.69 us
  transfers between devices with their start and end apart: 1, of which 0 were waited for; matrix products, arithmetic and copies ran while one was open for 4% of the time, Pallas kernels for 52%

profile of v1, /device:TPU:1, one launch (start us, length us, event | category | flops | bytes accessed | tf_op | source)
XLA Modules:
  0.0 248.0 jit_solution(10922448601300097988)
XLA Ops:
  7.2 0.0 all-gather.3.cloned.1.call-start
  7.2 1.3 copy.15
  8.5 24.5 %all_to_all.5 = bf16[16,128,256]{2,1,0:T(8,128)(2,1)} all-to-all(bf16[16,128,256]{2,1,0:T(8,128)(2,1)S(1)} %bitcast.15), channel_id=1, replica_groups=mesh['xl'=2,'co'=2,'z'=4,'y'=4,'xh'=2] {'z','y'}, dimensions={0} | all-to-all | bytes 2097152 | tf_op jit(solution)/shard_map/all_to_all | solution.py:395
  33.1 0.0 all-gather.3.cloned.1.call-update
  33.1 3.2 %copy.10 = bf16[4096,3,128]{0,2,1:T(8,128)(2,1)S(1)} copy(bf16[4096,3,128]{2,0,1:T(8,128)(2,1)} %param.6) | data formatting | bytes 6291456 | tf_op args[1]
  36.3 2.8 %copy.11.w_own = bf16[4096,384]{1,0:T(8,128)(2,1)} copy(bf16[4096,384]{0,1:T(8,128)(2,1)S(1)} %bitcast.14) | data formatting | bytes 6291456 | tf_op jit(solution)/shard_map/reshape | solution.py:386
  39.1 0.0 copy-start.1
  39.1 0.0 copy-start.2
  39.1 0.1 pad.6.clone
  39.2 1.9 fusion
  41.2 1.4 pad_maximum_fusion
  42.5 0.0 copy-done.1
  42.5 0.0 copy-done.2
  42.5 0.7 maximum_maximum_fusion.gains
  43.2 108.0 %qkv.1 = (bf16[2,1024,128]{2,1,0:T(8,128)(2,1)}, bf16[4,1024,128]{2,1,0:T(8,128)(2,1)}, bf16[4,1024,128]{2,1,0:T(8,128)(2,1)}, f32[2,2,1024]{2,1,0:T(2,128)}) custom-call(bf16[2,1024,128]{2,1,0:T(8,128)(2,1)} %tok.1, bf16[4096,384]{1,0:T(8,128)(2,1)} %copy.11.w_own, f32[8,128]{1,0:T(8,128)} %maximum_maximum_fusion.gains, ...), custom_call_target="tpu_custom_call" | custom-call | tf_op jit(solution)/shard_map/qkv/pallas_call | solution.py:403
  151.1 0.0 copy-start
  151.2 20.3 %attend.1 = (bf16[2,1024,128]{2,1,0:T(8,128)(2,1)}, f32[8,128]{1,0:T(8,128)}) custom-call(bf16[2,1024,128]{2,1,0:T(8,128)(2,1)} %get-tuple-element.11.q, bf16[4096,128]{1,0:T(8,128)(2,1)} %bitcast.18, bf16[4096,128]{1,0:T(8,128)(2,1)} %bitcast.19), custom_call_target="tpu_custom_call" | custom-call | tf_op jit(solution)/shard_map/attend/pallas_call | solution.py:437
  171.5 0.0 all-gather.3.cloned.1.call-done
  171.5 65.9 %mix.1 = (bf16[2,1024,128]{2,1,0:T(8,128)(2,1)}, f32[8,128]{1,0:T(8,128)}) custom-call(bf16[2,1024,128]{2,1,0:T(8,128)(2,1)} %get-tuple-element.14.o, f32[8,128]{1,0:T(8,128)} %get-tuple-element.15.top, bf16[4096,256]{1,0:T(8,128)(2,1)} %bitcast.16), custom_call_target="tpu_custom_call" | custom-call | tf_op jit(solution)/shard_map/mix/pallas_call | solution.py:449
  237.4 1.2 slice.3
  238.6 1.9 copy.18
  240.5 0.0 copy-done
  240.5 0.6 copy.19
  (3 shorter events, 0.0 us)
Async XLA Ops:
  7.2 164.3 %all-gather.3.cloned.1.call-start = ((), (), s32[]{:S(2)}) async-start(), calls=%async_computation.1 | async-start | bytes 3145728 | tf_op jit(solution)/shard_map/all_gather | solution.py:398
  39.1 3.4 %copy-start.1 = (f32[128]{0:T(128)S(1)}, f32[128]{0:T(128)}, u32[]{:S(2)}) copy-start(f32[128]{0:T(128)} %param.8) | copy-start | bytes 1540
  39.1 3.4 %copy-start.2 = (f32[128]{0:T(128)S(1)}, f32[128]{0:T(128)}, u32[]{:S(2)}) copy-start(f32[128]{0:T(128)} %param.7) | copy-start | bytes 1540
  151.1 89.4 %copy-start = (f32[2,2,1024]{2,1,0:T(2,128)S(1)}, f32[2,2,1024]{2,1,0:T(2,128)}, u32[]{:S(2)}) copy-start(f32[2,2,1024]{2,1,0:T(2,128)} %get-tuple-element.29) | copy-start | bytes 49156
Sparse Core Ops, SparseCore 0:
  33.2 41.4 all-gather.2

commit v2 on v0

v2 whole, which is shorter than its diff:
```python
import contextlib
import math

import jax
import jax.numpy as jnp
import numpy as np
from jax import lax
from jax.experimental import pallas as pl
from jax.experimental.pallas import tpu as pltpu
from jax.sharding import Mesh
from jax.sharding import PartitionSpec as P

EPS = 1e-06
ROPE_BASE = 500000.0
NEG = -1e30
MESH = pl.DeviceIdType.MESH
HEAD = 128
TOK = 1024
CHUNKS = 2
CROWS = TOK // CHUNKS
WIDTH = 4096
BK = 512
VMEM_CAP = 60 * 1024 * 1024
SCALE = HEAD ** (-0.5)
LOG2E = math.log2(math.e)
DIRS = (1, -1)
PART = {1: 0, -1: 1}


def scope(name):
    return contextlib.nullcontext()


def here():
    xh, xl = lax.axis_index("xh"), lax.axis_index("xl")
    return xh * 2 + xl, xh, xl, lax.axis_index("co"), lax.axis_index("z"), lax.axis_index("y")


def seq_of(x):
    return 1 - ((x + 1) // 2) % 2


def half_of(x):
    return 1 - x % 2


def at_x(x, core=None):
    dev = {"xl": x % 2, "xh": x // 2}
    if core is not None:
        dev["co"] = core
    return dev


class Sender:
    def __init__(self, ssem, rsem):
        self.ssem, self.rsem, self.sent = ssem, rsem, []

    def __call__(self, src, dst, dev):
        c = len(self.sent)
        cp = pltpu.make_async_remote_copy(
            src_ref=src,
            dst_ref=dst,
            send_sem=self.ssem.at[c],
            recv_sem=self.rsem.at[c],
            device_id=dev,
            device_id_type=MESH,
        )
        cp.start()
        self.sent.append(cp)
        return cp


class Gather:
    def __init__(self, buf, send, z, y, use):
        self.buf, self.send, self.use = buf, send, use
        self.first, self.second = (z, y), (y, z)
        self.p1, self.p1f, self.p2, self.p2f = {}, {}, {}, {}

    def place(self, h, f, s):
        return (f % 4, s % 4) if h == 0 else (s % 4, f % 4)

    def at(self, h, df, ds):
        return self.place(h, self.first[h] + df, self.second[h] + ds)

    def move(self, h, df, ds, part, along, d):
        zz, yy = self.at(h, df, ds)
        ref = self.buf.at[h, zz, yy] if part is None else self.buf.at[h, zz, yy, part]
        name = (("z", "y"), ("y", "z"))[h][along]
        me = (self.first[h], self.second[h])[along]
        return self.send(ref, ref, {name: (me + d + 4) % 4})

    def start(self, h):
        for d in DIRS:
            self.p1[h, d] = self.move(h, 0, 0, None, 0, d)

    def start_second(self, h):
        for d in DIRS:
            self.p2[h, 0, d] = self.move(h, 0, 0, None, 1, d)

    def own(self, h):
        self.use(h, *self.at(h, 0, 0))

    def near(self, h, d):
        self.p1[h, d].wait_recv()
        self.p1f[h, d] = self.move(h, 4 - d, 0, PART[d], 0, d)
        for e in DIRS:
            self.p2[h, -d, e] = self.move(h, 4 - d, 0, None, 1, e)

    def use_near(self, h, d):
        self.use(h, *self.at(h, 4 - d, 0))

    def pass_on(self, h, j):
        for d in DIRS:
            self.p2[h, j, d].wait_recv()
            self.p2f[h, j, d] = self.move(h, j + 4, 4 - d, PART[d], 1, d)

    def use_passed(self, h, j):
        for d in DIRS:
            self.use(h, *self.at(h, j + 4, 4 - d))

    def opposite(self, h):
        for d in DIRS:
            self.p1f[h, d].wait_recv()
        for d in DIRS:
            self.p2[h, 2, d] = self.move(h, 2, 0, None, 1, d)

    def use_opposite(self, h):
        self.use(h, *self.at(h, 2, 0))

    def last(self, h, j):
        for d in DIRS:
            self.p2f[h, j, d].wait_recv()
        self.use(h, *self.at(h, j + 4, 2))


def layer_kernel(
    tok, w_own, q_gain, k_gain, w_out, freq,
    mixed, peak, stat_out,
    buf, w_far, gains, gains_far, cosf, sinf, acc, acc_far, zb, yb, inv, inv_in,
    q_all, k_all, v_all, q_far, k_far, v_far,
    wz, w_cols, buf2, o_far, acc2, ob, tops,
    xs, xr, as_, ar, bs, br,
):
    x, xh, xl, co, z, y = here()
    right, left, pair, same = (x + 1) % 4, (x + 3) % 4, 3 - x, xh * 2 + (1 - xl)
    other = {"co": 1 - co}
    peers = (
        [at_x(right), at_x(left), other, at_x(right, 1 - co), at_x(left, 1 - co)]
        + [{"z": (z + i) % 4} for i in (1, 2, 3)]
        + [{"y": (y + i) % 4} for i in (1, 2, 3)]
    )
    with scope("greet"):
        barrier = pltpu.get_barrier_semaphore()
        for dev in peers:
            pl.semaphore_signal(barrier, inc=1, device_id=dev, device_id_type=MESH)
        pl.semaphore_wait(barrier, len(peers))
    send = Sender(xs, xr)
    mine = half_of(x) * 2 + co
    theirs = (1 - half_of(x)) * 2 + co
    me_seq = seq_of(x)
    sub = CROWS // 2

    toks = {}

    def send_tokens(ch):
        for h in (0, 1):
            rows = pl.ds(ch * CROWS + h * sub, sub)
            dst = buf.at[ch, h, z, y, xh]
            toks[ch, h] = (
                send(tok.at[xh, rows], dst, at_x(right)),
                send(tok.at[1 - xh, rows], dst, at_x(left)),
            )

    send_tokens(0)
    gains[0:1, :] = q_gain[...]
    gains[1:2, :] = k_gain[...]

    def w_rows(i):
        return pl.ds(pl.multiple_of((co * 2 + i) * 1024, 1024), 1024)

    far_w = [send(w_own.at[:, w_rows(0)], w_far.at[:, w_rows(0)], at_x(pair))]
    send_tokens(1)
    far_w.append(send(w_own.at[:, w_rows(1)], w_far.at[:, w_rows(1)], at_x(pair)))
    far_g = send(gains, gains_far, at_x(pair))
    relayed = {}

    def relay(i):
        far_w[i].wait_recv()
        relayed[i] = send(w_far.at[:, w_rows(i)], w_far.at[:, w_rows(i)], other)

    def dots(target, w, ch, h, blocks, zero=False):
        lhs, rhs = [], []
        for zz, yy in blocks:
            lhs += [buf[ch, h, zz, yy, 0], buf[ch, h, zz, yy, 1]]
            rows = pl.ds(pl.multiple_of((zz * 4 + yy) * 256, 256), 256)
            rhs.append(jnp.concatenate([w[0, rows, :], w[1, rows, :], w[2, rows, :]], axis=-1))
        lhs = jnp.concatenate(lhs, axis=-1)
        rhs = rhs[0] if len(rhs) == 1 else jnp.concatenate(rhs, axis=0)
        out = jnp.dot(lhs, rhs, preferred_element_type=jnp.float32)
        rows = pl.ds(ch * CROWS + h * sub, sub)
        target[rows, :] = out if zero else target[rows, :] + out

    def gather_of(ch):
        return Gather(
            buf.at[ch],
            Sender(as_.at[ch], ar.at[ch]),
            z,
            y,
            lambda h, zz, yy: dots(acc, w_own, ch, h, [(zz, yy)]),
        )

    def own_dot(ch, h):
        dots(acc, w_own, ch, h, [(z, y)], True)

    def far_dots(ch, zs):
        for i, zz in enumerate(zs):
            for h in (0, 1):
                dots(acc_far, w_far, ch, h, [(zz, yy) for yy in range(4)], zz == 0)

    def tables():
        def some(i, carry):
            rows = pl.ds(pl.multiple_of(i * 256, 256), 256)
            p = lax.broadcasted_iota(jnp.int32, (256, HEAD), 0) + (mine * TOK + i * 256)
            lane = lax.broadcasted_iota(jnp.int32, (256, HEAD), 1)
            angle = p.astype(jnp.float32) * freq[...]
            cosf[rows, :] = jnp.cos(angle)
            sine = jnp.sin(angle)
            sinf[rows, :] = jnp.where(lane < HEAD // 2, -sine, sine)
            return carry

        lax.fori_loop(0, TOK // 256, some, 0)

    got = {}

    def squares(ch):
        for j in (0, 1):
            cols = pl.ds(j * HEAD, HEAD)
            for i in range(2):
                rows = pl.ds(ch * CROWS + i * sub, sub)
                a, b = acc[rows, cols], acc_far[rows, cols]
                zb[ch, z, j : j + 1, i * sub : (i + 1) * sub] = jnp.sum(
                    (a * a + b * b).T, axis=0, keepdims=True
                )
        ref = zb.at[ch, z]
        got["z", ch] = [send(ref, ref, {"z": (z + i) % 4}) for i in (1, 2, 3)]

    def totals(ch):
        for cp in got["z", ch]:
            cp.wait_recv()
        yb[ch, y] = (zb[ch, 0] + zb[ch, 1]) + (zb[ch, 2] + zb[ch, 3])
        ref = yb.at[ch, y]
        got["y", ch] = [send(ref, ref, {"y": (y + i) % 4}) for i in (1, 2, 3)]

    stats = []

    def rope(ch):
        for cp in got["y", ch]:
            cp.wait_recv()
        inv[ch] = lax.rsqrt(((yb[ch, 0] + yb[ch, 1]) + (yb[ch, 2] + yb[ch, 3])) / WIDTH + EPS)
        for dev in (right, left):
            stats.append(send(inv.at[ch], inv_in.at[me_seq, ch], at_x(dev)))
        slot = mine * CHUNKS + ch
        for i in range(2):
            here_rows = slice(i * sub, (i + 1) * sub)
            rows = pl.ds(ch * CROWS + i * sub, sub)
            cs, sn = cosf[rows, :], sinf[rows, :]

            def turned(a, j, g):
                col = jnp.broadcast_to(inv[ch, j : j + 1, here_rows], (HEAD, sub)).T
                t = a[rows, j * HEAD : (j + 1) * HEAD] * col * g[j : j + 1, :]
                return (t * cs + pltpu.roll(t, HEAD // 2, 1) * sn).astype(jnp.bfloat16)

            q_far[rows, :] = turned(acc_far, 0, gains_far)
            k_far[rows, :] = turned(acc_far, 1, gains_far)
            v_far[ch, :, here_rows] = acc_far[rows, 2 * HEAD :].T.astype(jnp.bfloat16)
            q_all[0, rows, :] = turned(acc, 0, gains)
            k_all[slot, here_rows, :] = turned(acc, 1, gains)
            v_all[slot, :, here_rows] = acc[rows, 2 * HEAD :].T.astype(jnp.bfloat16)

    swaps, near = {}, []

    def swap(ch):
        rows = pl.ds(ch * CROWS, CROWS)
        slot = mine * CHUNKS + ch
        swaps[ch] = [
            send(k_far.at[rows], k_all.at[slot], at_x(pair)),
            send(v_far.at[ch], v_all.at[slot], at_x(pair)),
            send(q_far.at[rows], q_all.at[1, rows], at_x(pair, 1 - co)),
        ]
        near.append(send(k_all.at[slot], k_all.at[slot], other))
        near.append(send(v_all.at[slot], v_all.at[slot], other))

    def relay_kv(ch):
        slot = theirs * CHUNKS + ch
        for cp, ref in zip(swaps[ch], (k_all, v_all)):
            cp.wait_recv()
            near.append(send(ref.at[slot], ref.at[slot], other))

    part = pl.ds(pl.multiple_of(co * 64, 64), 64)

    def z_cols(zz):
        return pl.ds(pl.multiple_of((zz % 4) * 1024, 1024), 1024)

    def y_cols(yy):
        return pl.ds(pl.multiple_of((yy % 4) * 256, 256), 256)

    def cols_z():
        wz[z] = w_out[part, z_cols(z)]
        got["wz"] = [
            send(w_out.at[part, z_cols(z + i)], wz.at[z], {"z": (z + i) % 4}) for i in (1, 2, 3)
        ]

    def cols_y():
        for cp in got["wz"]:
            cp.wait_recv()
        w_cols[:, y, xh, part, :] = wz[:, :, y_cols(y)]
        got["wy"] = [
            send(wz.at[:, :, y_cols(y + i)], w_cols.at[:, y, xh, part], {"y": (y + i) % 4})
            for i in (1, 2, 3)
        ]

    def cols_x():
        for cp in got["wy"]:
            cp.wait_recv()
        ref = w_cols.at[:, :, xh, part]
        got["wx"] = [send(ref, ref, at_x(pair))]

    def cols_core():
        got["wx"][0].wait_recv()
        ref = w_cols.at[:, :, :, part]
        got["wc"] = [send(ref, ref, other)]

    g = [gather_of(0), gather_of(1)]

    def begin(ch):
        for h in (0, 1):
            for cp in toks[ch, h]:
                cp.wait_recv()
            g[ch].start(h)
        for h in (0, 1):
            g[ch].start_second(h)

    def middle(ch):
        for h in (0, 1):
            own_dot(ch, h)
        for d in DIRS:
            for h in (0, 1):
                g[ch].near(h, d)
        for d in DIRS:
            for h in (0, 1):
                g[ch].use_near(h, d)
        for h in (0, 1):
            g[ch].pass_on(h, 0)
        for h in (0, 1):
            g[ch].opposite(h)
        for h in (0, 1):
            g[ch].use_passed(h, 0)
            g[ch].use_opposite(h)
        for h in (0, 1):
            g[ch].pass_on(h, -1)
        for h in (0, 1):
            g[ch].use_passed(h, -1)
        for h in (0, 1):
            g[ch].pass_on(h, 1)

    def drain(ch, j):
        for h in (0, 1):
            g[ch].last(h, j)

    with scope("begin0"):
        begin(0)
    with scope("tables"):
        tables()
    with scope("middle0"):
        middle(0)
    with scope("begin1"):
        begin(1)
        for h in (0, 1):
            g[0].pass_on(h, 2)
        for h in (0, 1):
            g[0].use_passed(h, 1)
            g[0].use_passed(h, 2)
    with scope("drain0"):
        for j in (0, -1, 1, 2):
            drain(0, j)
        relay(0)
    with scope("middle1"):
        middle(1)
        for h in (0, 1):
            g[1].pass_on(h, 2)
    with scope("far0"):
        relayed[0].wait_recv()
        far_dots(0, (0, 2))
        for h in (0, 1):
            g[1].use_passed(h, 1)
    with scope("relay1"):
        relay(1)
    with scope("use2"):
        for h in (0, 1):
            g[1].use_passed(h, 2)
        relayed[1].wait_recv()
    with scope("far0b"):
        far_dots(0, (1, 3))
        squares(0)
    with scope("drain1"):
        for j in (0, -1):
            drain(1, j)
        totals(0)
        for j in (1, 2):
            drain(1, j)
        cols_z()
    with scope("far1"):
        far_dots(1, (0, 2, 1, 3))
        squares(1)
    far_g.wait_recv()
    with scope("rope0"):
        rope(0)
        swap(0)
    with scope("tot1"):
        totals(1)
        cols_y()
    with scope("rope1"):
        rope(1)
        swap(1)
    with scope("relay_kv"):
        for ch in range(CHUNKS):
            relay_kv(ch)
        cols_x()
    with scope("swap_wait"):
        for ch in range(CHUNKS):
            swaps[ch][2].wait_recv()
        for cp in near:
            cp.wait_recv()

    factor = SCALE * LOG2E
    best = [jnp.full((1, BK), NEG, jnp.float32)]

    def attend(which, ch):
        quarter = mine if which == 0 else (1 - half_of(x)) * 2 + (1 - co)
        qt = q_all[which, ch * CROWS : (ch + 1) * CROWS, :]

        def visit(j, state, masked):
            top, den, out = state
            s = lax.dot_general(
                k_all[j], qt, (((1,), (1,)), ((), ())), preferred_element_type=jnp.float32
            )
            if masked:
                r = lax.broadcasted_iota(jnp.int32, (BK, CROWS), 0)
                c = lax.broadcasted_iota(jnp.int32, (BK, CROWS), 1)
                s = jnp.where(r <= c, s, NEG)
            new = jnp.maximum(top, jnp.max(s, axis=0, keepdims=True))
            e = jnp.exp2((s - new) * factor)
            keep = jnp.exp2((top - new) * factor)
            den = den * keep + jnp.sum(e, axis=0, keepdims=True)
            out = out * keep + jnp.dot(
                v_all[j], e.astype(jnp.bfloat16), preferred_element_type=jnp.float32
            )
            return new, den, out

        state = (
            jnp.full((1, CROWS), NEG, jnp.float32),
            jnp.zeros((1, CROWS), jnp.float32),
            jnp.zeros((HEAD, CROWS), jnp.float32),
        )
        last = quarter * CHUNKS + ch
        state = lax.fori_loop(0, last, lambda j, st: visit(j, st, False), state)
        top, den, out = visit(last, state, True)
        best[0] = jnp.maximum(best[0], top)
        return (out / den).T.astype(jnp.bfloat16)

    back = {}

    def attend_half(h):
        o_far[h] = attend(1, h)
        back[h] = send(o_far.at[h], buf2.at[h, z, y, xh], at_x(pair, 1 - co))
        buf2[h, z, y, xh] = attend(0, h)

    def use2(h, zz, yy, zero=False):
        lhs = jnp.concatenate([buf2[h, zz, yy, 0], buf2[h, zz, yy, 1]], axis=-1)
        rhs = jnp.concatenate([w_cols[zz, yy, 0], w_cols[zz, yy, 1]], axis=0)
        out = jnp.dot(lhs, rhs, preferred_element_type=jnp.float32)
        rows = pl.ds(h * CROWS, CROWS)
        acc2[rows, :] = out if zero else acc2[rows, :] + out

    g2 = Gather(buf2, Sender(bs, br), z, y, use2)
    with scope("attend0"):
        attend_half(0)
    with scope("start2_0"):
        cols_core()
        back[0].wait_recv()
        g2.start(0)
        g2.start_second(0)
    with scope("attend1"):
        attend_half(1)
    with scope("start2_1"):
        place = xl * 2 + co
        tops[place] = jnp.broadcast_to(jnp.max(best[0], axis=1, keepdims=True), (8, HEAD)) * SCALE
        back[1].wait_recv()
        g2.start(1)
        g2.start_second(1)
        peaks = [
            send(tops.at[place], tops.at[place], dev)
            for dev in (other, at_x(same), at_x(same, 1 - co))
        ]
    with scope("near2"):
        for d in DIRS:
            g2.near(0, d)
        got["wc"][0].wait_recv()
        use2(0, z, y, True)
        for d in DIRS:
            g2.near(1, d)
        use2(1, z, y, True)
        for h in (0, 1):
            for d in DIRS:
                g2.use_near(h, d)
        for h in (0, 1):
            g2.pass_on(h, 0)
        for h in (0, 1):
            g2.opposite(h)
        for h in (0, 1):
            g2.use_passed(h, 0)
            g2.use_opposite(h)
    with scope("pass2"):
        for j in (-1, 1, 2):
            for h in (0, 1):
                g2.pass_on(h, j)
            for h in (0, 1):
                g2.use_passed(h, j)
    fin = []
    with scope("drain2"):
        for j in (0, -1, 1):
            for h in (0, 1):
                g2.last(h, j)
        for h in (0, 1):
            g2.last(h, 2)
            rows = pl.ds(h * CROWS, CROWS)
            for i in (0, 1):
                ob[i, rows, :] = acc2[rows, i * HEAD : (i + 1) * HEAD].astype(jnp.bfloat16)
            for dev in (right, left):
                fin.append(send(ob.at[dev // 2, rows], mixed.at[me_seq, rows], at_x(dev)))
    with scope("final"):
        for cp in peaks:
            cp.wait_recv()
        peak[...] = jnp.maximum(jnp.maximum(tops[0], tops[1]), jnp.maximum(tops[2], tops[3]))
        for cp in stats:
            cp.wait_recv()
        for s in (0, 1):
            for ch in range(CHUNKS):
                stat_out[:, s, ch * CROWS : (ch + 1) * CROWS] = inv_in[s, ch]
        for cp in fin:
            cp.wait_recv()
    with scope("wait_send"):
        for s in (send, g[0].send, g[1].send, g2.send):
            for cp in s.sent:
                cp.wait_send()


def vmem(count):
    return [pl.BlockSpec(memory_space=pltpu.VMEM)] * count


def shards(tokens, w_qkv, q_gain, k_gain, w_out):
    bf, f32 = jnp.bfloat16, jnp.float32
    dma = pltpu.SemaphoreType.DMA
    sub = CROWS // 2
    freq = ROPE_BASE ** (-(np.arange(HEAD) % (HEAD // 2) * 2.0) / HEAD)
    mixed, peak, stat = pl.pallas_call(
        layer_kernel,
        out_shape=(
            jax.ShapeDtypeStruct((2, TOK, HEAD), bf),
            jax.ShapeDtypeStruct((8, HEAD), f32),
            jax.ShapeDtypeStruct((2, 2, TOK), f32),
        ),
        in_specs=vmem(6),
        out_specs=tuple(vmem(3)),
        scratch_shapes=[
            pltpu.VMEM((CHUNKS, 2, 4, 4, 2, sub, HEAD), bf),
            pltpu.VMEM((3, WIDTH, HEAD), bf),
            pltpu.VMEM((8, HEAD), f32),
            pltpu.VMEM((8, HEAD), f32),
            pltpu.VMEM((TOK, HEAD), f32),
            pltpu.VMEM((TOK, HEAD), f32),
            pltpu.VMEM((TOK, 3 * HEAD), f32),
            pltpu.VMEM((TOK, 3 * HEAD), f32),
            pltpu.VMEM((CHUNKS, 4, 2, CROWS), f32),
            pltpu.VMEM((CHUNKS, 4, 2, CROWS), f32),
            pltpu.VMEM((CHUNKS, 2, CROWS), f32),
            pltpu.VMEM((2, CHUNKS, 2, CROWS), f32),
            pltpu.VMEM((2, TOK, HEAD), bf),
            pltpu.VMEM((4 * CHUNKS, CROWS, HEAD), bf),
            pltpu.VMEM((4 * CHUNKS, HEAD, CROWS), bf),
            pltpu.VMEM((TOK, HEAD), bf),
            pltpu.VMEM((TOK, HEAD), bf),
            pltpu.VMEM((CHUNKS, HEAD, CROWS), bf),
            pltpu.VMEM((4, 64, 1024), bf),
            pltpu.VMEM((4, 4, 2, HEAD, 256), bf),
            pltpu.VMEM((2, 4, 4, 2, CROWS, HEAD), bf),
            pltpu.VMEM((2, CROWS, HEAD), bf),
            pltpu.VMEM((TOK, 256), f32),
            pltpu.VMEM((2, TOK, HEAD), bf),
            pltpu.VMEM((4, 8, HEAD), f32),
            dma((72,)),
            dma((72,)),
            dma((CHUNKS, 40)),
            dma((CHUNKS, 40)),
            dma((40,)),
            dma((40,)),
        ],
        compiler_params=pltpu.CompilerParams(
            collective_id=0, has_side_effects=True, vmem_limit_bytes=VMEM_CAP
        ),
        name="layer",
    )(
        tokens,
        w_qkv.transpose(1, 0, 2),
        q_gain[None],
        k_gain[None],
        w_out,
        jnp.asarray(freq[None], f32),
    )
    return mixed, peak[0, :1], stat


def solution(mesh):
    finer = Mesh(mesh.devices.reshape(2, 2, 4, 4, 2), ("xl", "co", "z", "y", "xh"))
    tensor = ("z", "y", "xh")
    seq = ("xl", "co")
    placed = (P(None, seq, tensor), P(None, None, tensor), P(tensor), P(tensor), P(tensor, None))
    return jax.shard_map(
        shards,
        mesh=finer,
        in_specs=placed,
        out_specs=(P(None, seq, tensor), P(tensor), P(None, None, seq)),
        check_vma=False,
    )
```

time: 594 us -> 169 us (0.28)
  waiting for transfers between devices: 488 us -> 0 us
  Pallas kernels: 0 us -> 163 us
  matrix products: 43.7 us -> 0 us
  other arithmetic: 17.4 us -> 0 us
  local copies, waits for them, and re-layouts: 18.1 us -> 4.38 us
  between operations: 14 us -> 0.64 us
  blocking collectives: 6.36 us -> 0 us
    all_gather x2 -> x0, waiting for transfers between devices: 253 us -> none  [the longest x1 205 us: shards(): lax.all_gather(tokens, TENSOR, axis=2, tiled=True).reshape(rows, width)]
    reduce_scatter x2 -> x0, waiting for transfers between devices: 218 us -> none  [sum_by_axis(): array = lax.psum_scatter(array, axis, scatter_dimension=dim, tiled=True)]
    pallas_call x0 -> x1, Pallas kernels: none -> 163 us  [shards(): pl.pallas_call(layer_kernel, out_shape=(jax.ShapeDtypeStruct((2, TOK, HEA...]
    dot_general x7 -> x0, matrix products: 43.7 us -> none  [the longest x1 11.3 us: shards(): jnp.dot(whole, flat_w[:, 2 * dloc:], preferred_element_type=jnp.float32)]
    unnamed x6 -> x0, waiting for transfers between devices: 16.1 us -> none
    unnamed x13 -> x2, local copies, waits for them, and re-layouts: 11.2 us -> 3.19 us
    all_to_all x1 -> x0, blocking collectives: 6.36 us -> none  [sent_to_all(): lax.all_to_all(jnp.broadcast_to(array[None], (size, *array.shape)), axis,...]
    reduce_sum x4 -> x0, other arithmetic: 6.33 us -> none  [the longest x2 4.51 us: online_update(): jnp.sum(weights, -1)]
  transfers between devices with their start and end apart: 6 -> 0, of which waited for: 6 -> 0; matrix products, arithmetic and copies ran while one was open for 4% -> 0% of each run, Pallas kernels for 0% -> 0%
where the time goes in v2:
time: 169 us; the launch traced here: 168 us
  Pallas kernels  163 us (96%)
  local copies, waits for them, and re-layouts  4.38 us (3%)
    pallas_call x1, Pallas kernels, shards(): pl.pallas_call(layer_kernel, out_shape=(jax.ShapeDtypeStruct((2, TOK, HEA...  163 us

profile of v2, /device:TPU:1, one launch (start us, length us, event | category | flops | bytes accessed | tf_op | source)
XLA Modules:
  0.0 168.0 jit_solution(13938085906902567315)
XLA Ops:
  0.6 163.0 %layer.1 = (bf16[2,1024,128]{2,1,0:T(8,128)(2,1)}, f32[8,128]{1,0:T(8,128)}, f32[2,2,1024]{2,1,0:T(2,128)}) custom-call(bf16[2,1024,128]{2,1,0:T(8,128)(2,1)} %tok.1, bf16[3,4096,128]{2,1,0:T(8,128)(2,1)} %bitcast.4, f32[1,128]{1,0:T(1,128)} %bitcast.5, f32[1,128]{1,0:T(1,128)} %bitcast.6, bf16[128,4096]{1,0:T(8,128)(2,1)} %w_out.1, f32[1,128]{1,0:T(1,128)} %constant.2.clone.freq), custom_call_target="tpu_custom_call" | custom-call | tf_op jit(solution)/shard_map/layer/pallas_call | solution.py:567
  163.7 1.2 slice.3
  164.8 1.9 %copy.11 = bf16[2,1024,128]{2,1,0:T(8,128)(2,1)} copy(bf16[2,1024,128]{2,1,0:T(8,128)(2,1)} %get-tuple-element.12) | data formatting | bytes 1048576
  166.7 1.3 copy.12

commit v3 on v2

--- a/solution.py
+++ b/solution.py
@@ -25,6 +25,7 @@
 LOG2E = math.log2(math.e)
 DIRS = (1, -1)
 PART = {1: 0, -1: 1}
+CQ, CV, CK = 0, HEAD, 2 * HEAD
 
 
 def scope(name):
@@ -89,29 +90,28 @@
         me = (self.first[h], self.second[h])[along]
         return self.send(ref, ref, {name: (me + d + 4) % 4})
 
-    def start(self, h):
-        for d in DIRS:
-            self.p1[h, d] = self.move(h, 0, 0, None, 0, d)
-
-    def start_second(self, h):
-        for d in DIRS:
-            self.p2[h, 0, d] = self.move(h, 0, 0, None, 1, d)
+    def start(self, h, part=None):
+        for d in DIRS:
+            self.p1.setdefault((h, d), []).append(self.move(h, 0, 0, part, 0, d))
+            self.p2.setdefault((h, 0, d), []).append(self.move(h, 0, 0, part, 1, d))
 
     def own(self, h):
         self.use(h, *self.at(h, 0, 0))
 
     def near(self, h, d):
-        self.p1[h, d].wait_recv()
+        for cp in self.p1[h, d]:
+            cp.wait_recv()
         self.p1f[h, d] = self.move(h, 4 - d, 0, PART[d], 0, d)
         for e in DIRS:
-            self.p2[h, -d, e] = self.move(h, 4 - d, 0, None, 1, e)
+            self.p2[h, -d, e] = [self.move(h, 4 - d, 0, None, 1, e)]
 
     def use_near(self, h, d):
         self.use(h, *self.at(h, 4 - d, 0))
 
     def pass_on(self, h, j):
         for d in DIRS:
-            self.p2[h, j, d].wait_recv()
+            for cp in self.p2[h, j, d]:
+                cp.wait_recv()
             self.p2f[h, j, d] = self.move(h, j + 4, 4 - d, PART[d], 1, d)
 
     def use_passed(self, h, j):
@@ -122,7 +122,7 @@
         for d in DIRS:
             self.p1f[h, d].wait_recv()
         for d in DIRS:
-            self.p2[h, 2, d] = self.move(h, 2, 0, None, 1, d)
+            self.p2[h, 2, d] = [self.move(h, 2, 0, None, 1, d)]
 
     def use_opposite(self, h):
         self.use(h, *self.at(h, 2, 0))
@@ -134,13 +134,20 @@
 
 
 def layer_kernel(
-    tok, w_own, q_gain, k_gain, w_out, freq,
+    tok_hbm, w_hbm, q_gain, k_gain, w_out_hbm, freq,
     mixed, peak, stat_out,
-    buf, w_far, gains, gains_far, cosf, sinf, acc, acc_far, zb, yb, inv, inv_in,
+    tok, w_own, w_out, buf, w_far, gains, gains_far, cosf, sinf, acc, acc_far, zb, yb, inv, inv_in,
     q_all, k_all, v_all, q_far, k_far, v_far,
-    wz, w_cols, buf2, o_far, acc2, ob, tops,
-    xs, xr, as_, ar, bs, br,
+    wz, w_cols, buf2, o_far, acc2, ob, tops, inv_far,
+    sc0, sc1, top_r, den_r, acc_r, pace,
+    xs, xr, as_, ar, bs, br, ins,
 ):
+    loads = [
+        pltpu.make_async_copy(src, dst, ins.at[i])
+        for i, (src, dst) in enumerate(((tok_hbm, tok), (w_hbm, w_own), (w_out_hbm, w_out)))
+    ]
+    for cp in loads:
+        cp.start()
     x, xh, xl, co, z, y = here()
     right, left, pair, same = (x + 1) % 4, (x + 3) % 4, 3 - x, xh * 2 + (1 - xl)
     other = {"co": 1 - co}
@@ -171,34 +178,40 @@
                 send(tok.at[1 - xh, rows], dst, at_x(left)),
             )
 
+    loads[0].wait()
     send_tokens(0)
     gains[0:1, :] = q_gain[...]
     gains[1:2, :] = k_gain[...]
-
-    def w_rows(i):
-        return pl.ds(pl.multiple_of((co * 2 + i) * 1024, 1024), 1024)
-
-    far_w = [send(w_own.at[:, w_rows(0)], w_far.at[:, w_rows(0)], at_x(pair))]
+    loads[1].wait()
+
+    w_rows = pl.ds(pl.multiple_of(co * 2048, 2048), 2048)
+    far_w, relayed = {}, {}
+
+    def send_w(j):
+        far_w[j] = send(w_own.at[j, w_rows], w_far.at[j, w_rows], at_x(pair))
+
+    def relay(j):
+        far_w[j].wait_recv()
+        relayed[j] = send(w_far.at[j, w_rows], w_far.at[j, w_rows], other)
+
+    send_w(0)
     send_tokens(1)
-    far_w.append(send(w_own.at[:, w_rows(1)], w_far.at[:, w_rows(1)], at_x(pair)))
+    send_w(2)
+    send_w(1)
     far_g = send(gains, gains_far, at_x(pair))
-    relayed = {}
-
-    def relay(i):
-        far_w[i].wait_recv()
-        relayed[i] = send(w_far.at[:, w_rows(i)], w_far.at[:, w_rows(i)], other)
-
-    def dots(target, w, ch, h, blocks, zero=False):
+
+    def dots(target, w, ch, h, blocks, zero=False, kinds=(0, 2, 1), at=0):
         lhs, rhs = [], []
         for zz, yy in blocks:
             lhs += [buf[ch, h, zz, yy, 0], buf[ch, h, zz, yy, 1]]
             rows = pl.ds(pl.multiple_of((zz * 4 + yy) * 256, 256), 256)
-            rhs.append(jnp.concatenate([w[0, rows, :], w[1, rows, :], w[2, rows, :]], axis=-1))
+            some = [w[j, rows, :] for j in kinds]
+            rhs.append(some[0] if len(some) == 1 else jnp.concatenate(some, axis=-1))
         lhs = jnp.concatenate(lhs, axis=-1)
         rhs = rhs[0] if len(rhs) == 1 else jnp.concatenate(rhs, axis=0)
         out = jnp.dot(lhs, rhs, preferred_element_type=jnp.float32)
-        rows = pl.ds(ch * CROWS + h * sub, sub)
-        target[rows, :] = out if zero else target[rows, :] + out
+        place = (pl.ds(ch * CROWS + h * sub, sub), slice(at, at + HEAD * len(kinds)))
+        target[place] = out if zero else target[place] + out
 
     def gather_of(ch):
         return Gather(
@@ -212,10 +225,11 @@
     def own_dot(ch, h):
         dots(acc, w_own, ch, h, [(z, y)], True)
 
-    def far_dots(ch, zs):
-        for i, zz in enumerate(zs):
+    def far_dots(ch, kinds, at):
+        for zz in range(4):
             for h in (0, 1):
-                dots(acc_far, w_far, ch, h, [(zz, yy) for yy in range(4)], zz == 0)
+                blocks = [(zz, yy) for yy in range(4)]
+                dots(acc_far, w_far, ch, h, blocks, zz == 0, kinds, at)
 
     def tables():
         def some(i, carry):
@@ -233,8 +247,8 @@
     got = {}
 
     def squares(ch):
-        for j in (0, 1):
-            cols = pl.ds(j * HEAD, HEAD)
+        for j, c in ((0, CQ), (1, CK)):
+            cols = pl.ds(c, HEAD)
             for i in range(2):
                 rows = pl.ds(ch * CROWS + i * sub, sub)
                 a, b = acc[rows, cols], acc_far[rows, cols]
@@ -251,50 +265,62 @@
         ref = yb.at[ch, y]
         got["y", ch] = [send(ref, ref, {"y": (y + i) % 4}) for i in (1, 2, 3)]
 
-    stats = []
-
-    def rope(ch):
-        for cp in got["y", ch]:
-            cp.wait_recv()
-        inv[ch] = lax.rsqrt(((yb[ch, 0] + yb[ch, 1]) + (yb[ch, 2] + yb[ch, 3])) / WIDTH + EPS)
-        for dev in (right, left):
-            stats.append(send(inv.at[ch], inv_in.at[me_seq, ch], at_x(dev)))
+    stats, invs = [], []
+    swaps, near = {}, []
+
+    def turned(a, j, g, rows, col=None):
+        t = a[rows, CK : CK + HEAD] if j else a[rows, CQ : CQ + HEAD]
+        if col is not None:
+            t = t * col
+        t = t * g[j : j + 1, :]
+        return (t * cosf[rows, :] + pltpu.roll(t, HEAD // 2, 1) * sinf[rows, :]).astype(jnp.bfloat16)
+
+    def early(ch):
         slot = mine * CHUNKS + ch
+        whole = pl.ds(ch * CROWS, CROWS)
         for i in range(2):
             here_rows = slice(i * sub, (i + 1) * sub)
             rows = pl.ds(ch * CROWS + i * sub, sub)
-            cs, sn = cosf[rows, :], sinf[rows, :]
-
-            def turned(a, j, g):
-                col = jnp.broadcast_to(inv[ch, j : j + 1, here_rows], (HEAD, sub)).T
-                t = a[rows, j * HEAD : (j + 1) * HEAD] * col * g[j : j + 1, :]
-                return (t * cs + pltpu.roll(t, HEAD // 2, 1) * sn).astype(jnp.bfloat16)
-
-            q_far[rows, :] = turned(acc_far, 0, gains_far)
-            k_far[rows, :] = turned(acc_far, 1, gains_far)
-            v_far[ch, :, here_rows] = acc_far[rows, 2 * HEAD :].T.astype(jnp.bfloat16)
-            q_all[0, rows, :] = turned(acc, 0, gains)
-            k_all[slot, here_rows, :] = turned(acc, 1, gains)
-            v_all[slot, :, here_rows] = acc[rows, 2 * HEAD :].T.astype(jnp.bfloat16)
-
-    swaps, near = {}, []
-
-    def swap(ch):
-        rows = pl.ds(ch * CROWS, CROWS)
+            v_far[ch, :, here_rows] = acc_far[rows, CV : CV + HEAD].T.astype(jnp.bfloat16)
+        swaps["v", ch] = send(v_far.at[ch], v_all.at[slot], at_x(pair))
+        for i in range(2):
+            rows = pl.ds(ch * CROWS + i * sub, sub)
+            q_far[rows, :] = turned(acc_far, 0, gains_far, rows)
+        swaps["q", ch] = send(q_far.at[whole], q_all.at[1, whole], at_x(pair, 1 - co))
+        for i in range(2):
+            here_rows = slice(i * sub, (i + 1) * sub)
+            rows = pl.ds(ch * CROWS + i * sub, sub)
+            q_all[0, rows, :] = turned(acc, 0, gains, rows)
+            v_all[slot, :, here_rows] = acc[rows, CV : CV + HEAD].T.astype(jnp.bfloat16)
+        near.append(send(v_all.at[slot], v_all.at[slot], other))
+
+    def late(ch):
+        for cp in got["y", ch]:
+            cp.wait_recv()
+        inv[ch] = lax.rsqrt(((yb[ch, 0] + yb[ch, 1]) + (yb[ch, 2] + yb[ch, 3])) / WIDTH + EPS)
         slot = mine * CHUNKS + ch
-        swaps[ch] = [
-            send(k_far.at[rows], k_all.at[slot], at_x(pair)),
-            send(v_far.at[ch], v_all.at[slot], at_x(pair)),
-            send(q_far.at[rows], q_all.at[1, rows], at_x(pair, 1 - co)),
-        ]
+        whole = pl.ds(ch * CROWS, CROWS)
+        cols = []
+        for i in range(2):
+            here_rows = slice(i * sub, (i + 1) * sub)
+            rows = pl.ds(ch * CROWS + i * sub, sub)
+            cols.append(jnp.broadcast_to(inv[ch, 1:2, here_rows], (HEAD, sub)).T)
+            k_far[rows, :] = turned(acc_far, 1, gains_far, rows, cols[i])
+        swaps["k", ch] = send(k_far.at[whole], k_all.at[slot], at_x(pair))
+        invs.append(send(inv.at[ch], inv_far.at[ch], at_x(pair, 1 - co)))
+        for i in range(2):
+            here_rows = slice(i * sub, (i + 1) * sub)
+            rows = pl.ds(ch * CROWS + i * sub, sub)
+            k_all[slot, here_rows, :] = turned(acc, 1, gains, rows, cols[i])
         near.append(send(k_all.at[slot], k_all.at[slot], other))
-        near.append(send(v_all.at[slot], v_all.at[slot], other))
-
-    def relay_kv(ch):
+        for dev in (right, left):
+            stats.append(send(inv.at[ch], inv_in.at[me_seq, ch], at_x(dev)))
+
+    def relay_kv(name, ch):
         slot = theirs * CHUNKS + ch
-        for cp, ref in zip(swaps[ch], (k_all, v_all)):
-            cp.wait_recv()
-            near.append(send(ref.at[slot], ref.at[slot], other))
+        ref = k_all if name == "k" else v_all
+        swaps[name, ch].wait_recv()
+        near.append(send(ref.at[slot], ref.at[slot], other))
 
     part = pl.ds(pl.multiple_of(co * 64, 64), 64)
 
@@ -319,16 +345,18 @@
             for i in (1, 2, 3)
         ]
 
-    def cols_x():
+    def cols_y_done():
         for cp in got["wy"]:
             cp.wait_recv()
-        ref = w_cols.at[:, :, xh, part]
-        got["wx"] = [send(ref, ref, at_x(pair))]
-
-    def cols_core():
-        got["wx"][0].wait_recv()
-        ref = w_cols.at[:, :, :, part]
-        got["wc"] = [send(ref, ref, other)]
+
+    def cols_x(i):
+        ref = w_cols.at[2 * i : 2 * i + 2, :, xh, part]
+        got["wx", i] = send(ref, ref, at_x(pair))
+
+    def cols_core(i):
+        got["wx", i].wait_recv()
+        ref = w_cols.at[2 * i : 2 * i + 2, :, :, part]
+        got["wc", i] = send(ref, ref, other)
 
     g = [gather_of(0), gather_of(1)]
 
@@ -337,8 +365,6 @@
             for cp in toks[ch, h]:
                 cp.wait_recv()
             g[ch].start(h)
-        for h in (0, 1):
-            g[ch].start_second(h)
 
     def middle(ch):
         for h in (0, 1):
@@ -375,105 +401,155 @@
         middle(0)
     with scope("begin1"):
         begin(1)
+    with scope("pass0"):
         for h in (0, 1):
             g[0].pass_on(h, 2)
         for h in (0, 1):
             g[0].use_passed(h, 1)
+        for h in (0, 1):
+            own_dot(1, h)
+    with scope("near1"):
+        for d in DIRS:
+            for h in (0, 1):
+                g[1].near(h, d)
+    with scope("drain0"):
+        for h in (0, 1):
             g[0].use_passed(h, 2)
-    with scope("drain0"):
-        for j in (0, -1, 1, 2):
+        for j in (0, -1, 1):
             drain(0, j)
+    with scope("middle1"):
+        for h in (0, 1):
+            g[1].pass_on(h, 0)
+        drain(0, 2)
+        for d in DIRS:
+            for h in (0, 1):
+                g[1].use_near(h, d)
+        for h in (0, 1):
+            g[1].opposite(h)
         relay(0)
-    with scope("middle1"):
-        middle(1)
+    with scope("mid1"):
+        for h in (0, 1):
+            g[1].use_passed(h, 0)
+            g[1].use_opposite(h)
+        for h in (0, 1):
+            g[1].pass_on(h, -1)
+        relay(2)
+        for h in (0, 1):
+            g[1].use_passed(h, -1)
+    with scope("pass1"):
+        for h in (0, 1):
+            g[1].pass_on(h, 1)
+        for h in (0, 1):
+            g[1].use_passed(h, 1)
+        for j in (0, 2):
+            relayed[j].wait_recv()
+        far_g.wait_recv()
+    with scope("far_qv0"):
+        far_dots(0, (0, 2), 0)
+    with scope("pass1b"):
         for h in (0, 1):
             g[1].pass_on(h, 2)
-    with scope("far0"):
-        relayed[0].wait_recv()
-        far_dots(0, (0, 2))
-        for h in (0, 1):
-            g[1].use_passed(h, 1)
-    with scope("relay1"):
+    with scope("early0"):
+        early(0)
+        for h in (0, 1):
+            g[1].use_passed(h, 2)
+    with scope("drain1"):
+        for j in (0, -1, 1):
+            drain(1, j)
+    with scope("relay_k"):
         relay(1)
-    with scope("use2"):
-        for h in (0, 1):
-            g[1].use_passed(h, 2)
+    with scope("drain1b"):
+        drain(1, 2)
+    with scope("far_qv1"):
+        far_dots(1, (0, 2), 0)
+    with scope("early1"):
+        early(1)
         relayed[1].wait_recv()
-    with scope("far0b"):
-        far_dots(0, (1, 3))
+    with scope("far_k"):
+        far_dots(0, (1,), CK)
         squares(0)
-    with scope("drain1"):
-        for j in (0, -1):
-            drain(1, j)
+        far_dots(1, (1,), CK)
+        squares(1)
+    with scope("tot"):
         totals(0)
-        for j in (1, 2):
-            drain(1, j)
+        totals(1)
+        loads[2].wait()
         cols_z()
-    with scope("far1"):
-        far_dots(1, (0, 2, 1, 3))
-        squares(1)
-    far_g.wait_recv()
-    with scope("rope0"):
-        rope(0)
-        swap(0)
-    with scope("tot1"):
-        totals(1)
+        relay_kv("v", 0)
+    with scope("late"):
+        late(0)
+        late(1)
+    with scope("relay_kv"):
+        relay_kv("v", 1)
         cols_y()
-    with scope("rope1"):
-        rope(1)
-        swap(1)
-    with scope("relay_kv"):
-        for ch in range(CHUNKS):
-            relay_kv(ch)
-        cols_x()
+        relay_kv("k", 0)
+        relay_kv("k", 1)
     with scope("swap_wait"):
         for ch in range(CHUNKS):
-            swaps[ch][2].wait_recv()
-        for cp in near:
-            cp.wait_recv()
-
-    factor = SCALE * LOG2E
-    best = [jnp.full((1, BK), NEG, jnp.float32)]
-
-    def attend(which, ch):
-        quarter = mine if which == 0 else (1 - half_of(x)) * 2 + (1 - co)
-        qt = q_all[which, ch * CROWS : (ch + 1) * CROWS, :]
-
-        def visit(j, state, masked):
-            top, den, out = state
-            s = lax.dot_general(
-                k_all[j], qt, (((1,), (1,)), ((), ())), preferred_element_type=jnp.float32
+            swaps["q", ch].wait_recv()
+        for cp in invs + near:
+            cp.wait_recv()
+
+    far_quarter = (1 - half_of(x)) * 2 + (1 - co)
+    back = {}
+
+    def attend(ch):
+        total = 6 + 2 * (ch + 1)
+        count = far_quarter * CHUNKS + ch + 1
+        rows = slice(ch * CROWS, (ch + 1) * CROWS)
+        for i, r in enumerate((inv, inv_far)):
+            pace[i] = r[ch, 0:1, :] * (SCALE * LOG2E)
+        top_r[...] = jnp.full((2, 1, CROWS), NEG, jnp.float32)
+        den_r[...] = jnp.zeros((2, 1, CROWS), jnp.float32)
+        acc_r[...] = jnp.zeros((2, HEAD, CROWS), jnp.float32)
+
+        def where(t):
+            own = (t + 16 - count) // 16
+            return 1 - own, (1 - own) * (count - 1 - t) + own * (t - count)
+
+        def score(t, into):
+            which, j = where(t)
+            into[...] = lax.dot_general(
+                k_all[j], q_all[which, rows, :], (((1,), (1,)), ((), ())),
+                preferred_element_type=jnp.float32,
             )
+
+        def weigh(t, cur, masked):
+            which, j = where(t)
+            s = cur[...]
             if masked:
                 r = lax.broadcasted_iota(jnp.int32, (BK, CROWS), 0)
                 c = lax.broadcasted_iota(jnp.int32, (BK, CROWS), 1)
                 s = jnp.where(r <= c, s, NEG)
+            top, p = top_r[which], pace[which]
             new = jnp.maximum(top, jnp.max(s, axis=0, keepdims=True))
-            e = jnp.exp2((s - new) * factor)
-            keep = jnp.exp2((top - new) * factor)
-            den = den * keep + jnp.sum(e, axis=0, keepdims=True)
-            out = out * keep + jnp.dot(
+            e = jnp.exp2((s - new) * p)
+            keep = jnp.exp2((top - new) * p)
+            den_r[which] = den_r[which] * keep + jnp.sum(e, axis=0, keepdims=True)
+            acc_r[which] = acc_r[which] * keep + jnp.dot(
                 v_all[j], e.astype(jnp.bfloat16), preferred_element_type=jnp.float32
             )
-            return new, den, out
-
-        state = (
-            jnp.full((1, CROWS), NEG, jnp.float32),
-            jnp.zeros((1, CROWS), jnp.float32),
-            jnp.zeros((HEAD, CROWS), jnp.float32),
-        )
-        last = quarter * CHUNKS + ch
-        state = lax.fori_loop(0, last, lambda j, st: visit(j, st, False), state)
-        top, den, out = visit(last, state, True)
-        best[0] = jnp.maximum(best[0], top)
-        return (out / den).T.astype(jnp.bfloat16)
-
-    back = {}
-
-    def attend_half(h):
-        o_far[h] = attend(1, h)
-        back[h] = send(o_far.at[h], buf2.at[h, z, y, xh], at_x(pair, 1 - co))
-        buf2[h, z, y, xh] = attend(0, h)
+            top_r[which] = new
+
+        score(0, sc0)
+        score(1, sc1)
+        weigh(0, sc0, True)
+
+        def two(i, carry):
+            t = 2 * i + 1
+            score(t + 1, sc0)
+            weigh(t, sc1, False)
+            score(t + 2, sc1)
+            weigh(t + 1, sc0, False)
+            return carry
+
+        lax.fori_loop(0, (total - 2) // 2, two, 0)
+        weigh(total - 1, sc1, True)
+        o_far[ch] = (acc_r[1] / den_r[1]).T.astype(jnp.bfloat16)
+        back[ch] = send(o_far.at[ch], buf2.at[ch, z, y, xh], at_x(pair, 1 - co))
+        buf2[ch, z, y, xh] = (acc_r[0] / den_r[0]).T.astype(jnp.bfloat16)
+        peaks_here = [jnp.max(top_r[i] * pace[i], axis=1, keepdims=True) for i in (0, 1)]
+        return jnp.maximum(*peaks_here) * (1 / LOG2E)
 
     def use2(h, zz, yy, zero=False):
         lhs = jnp.concatenate([buf2[h, zz, yy, 0], buf2[h, zz, yy, 1]], axis=-1)
@@ -484,48 +560,66 @@
 
     g2 = Gather(buf2, Sender(bs, br), z, y, use2)
     with scope("attend0"):
-        attend_half(0)
+        best = [attend(0)]
+        g2.start(0, xh)
+    with scope("attend1"):
+        best.append(attend(1))
+        g2.start(1, xh)
     with scope("start2_0"):
-        cols_core()
         back[0].wait_recv()
-        g2.start(0)
-        g2.start_second(0)
-    with scope("attend1"):
-        attend_half(1)
+        g2.start(0, 1 - xh)
+        cols_y_done()
+        cols_x(0)
+        cols_x(1)
     with scope("start2_1"):
+        back[1].wait_recv()
+        g2.start(1, 1 - xh)
         place = xl * 2 + co
-        tops[place] = jnp.broadcast_to(jnp.max(best[0], axis=1, keepdims=True), (8, HEAD)) * SCALE
-        back[1].wait_recv()
-        g2.start(1)
-        g2.start_second(1)
+        tops[place] = jnp.broadcast_to(jnp.maximum(*best), (8, HEAD))
         peaks = [
             send(tops.at[place], tops.at[place], dev)
             for dev in (other, at_x(same), at_x(same, 1 - co))
         ]
-    with scope("near2"):
+    with scope("near2_0"):
         for d in DIRS:
             g2.near(0, d)
-        got["wc"][0].wait_recv()
-        use2(0, z, y, True)
+    with scope("near2_1"):
         for d in DIRS:
             g2.near(1, d)
-        use2(1, z, y, True)
-        for h in (0, 1):
-            for d in DIRS:
-                g2.use_near(h, d)
-        for h in (0, 1):
-            g2.pass_on(h, 0)
-        for h in (0, 1):
-            g2.opposite(h)
-        for h in (0, 1):
-            g2.use_passed(h, 0)
+        cols_core(0)
+    with scope("pass2_0"):
+        g2.pass_on(0, 0)
+        g2.opposite(0)
+        g2.pass_on(1, 0)
+        g2.opposite(1)
+        cols_core(1)
+    with scope("pass2_1"):
+        g2.pass_on(0, -1)
+        for i in (0, 1):
+            got["wc", i].wait_recv()
+        for h in (0, 1):
+            use2(h, z, y, True)
+        for d in DIRS:
+            g2.use_near(0, d)
+        g2.pass_on(1, -1)
+        for d in DIRS:
+            g2.use_near(1, d)
+        g2.use_passed(0, 0)
+    with scope("mid2"):
+        g2.pass_on(0, 1)
+        g2.use_passed(1, 0)
+        for h in (0, 1):
             g2.use_opposite(h)
+        g2.pass_on(1, 1)
+        for h in (0, 1):
+            g2.use_passed(h, -1)
     with scope("pass2"):
-        for j in (-1, 1, 2):
-            for h in (0, 1):
-                g2.pass_on(h, j)
-            for h in (0, 1):
-                g2.use_passed(h, j)
+        g2.pass_on(0, 2)
+        g2.use_passed(0, 1)
+        g2.pass_on(1, 2)
+        g2.use_passed(1, 1)
+        for h in (0, 1):
+            g2.use_passed(h, 2)
     fin = []
     with scope("drain2"):
         for j in (0, -1, 1):
@@ -553,6 +647,12 @@
         for s in (send, g[0].send, g[1].send, g2.send):
             for cp in s.sent:
                 cp.wait_send()
+
+
+def finish_kernel(mixed, peak, stat, mixed_out, peak_out, stat_out):
+    mixed_out[...] = mixed[...]
+    peak_out[0] = peak[0, 0]
+    stat_out[...] = stat[...]
 
 
 def vmem(count):
@@ -571,9 +671,15 @@
             jax.ShapeDtypeStruct((8, HEAD), f32),
             jax.ShapeDtypeStruct((2, 2, TOK), f32),
         ),
-        in_specs=vmem(6),
+        in_specs=[
+            pl.BlockSpec(memory_space=pltpu.VMEM if small else pl.ANY)
+            for small in (False, False, True, True, False, True)
+        ],
         out_specs=tuple(vmem(3)),
         scratch_shapes=[
+            pltpu.VMEM((2, TOK, HEAD), bf),
+            pltpu.VMEM((3, WIDTH, HEAD), bf),
+            pltpu.VMEM((HEAD, WIDTH), bf),
             pltpu.VMEM((CHUNKS, 2, 4, 4, 2, sub, HEAD), bf),
             pltpu.VMEM((3, WIDTH, HEAD), bf),
             pltpu.VMEM((8, HEAD), f32),
@@ -599,12 +705,20 @@
             pltpu.VMEM((TOK, 256), f32),
             pltpu.VMEM((2, TOK, HEAD), bf),
             pltpu.VMEM((4, 8, HEAD), f32),
+            pltpu.VMEM((CHUNKS, 2, CROWS), f32),
+            pltpu.VMEM((BK, CROWS), f32),
+            pltpu.VMEM((BK, CROWS), f32),
+            pltpu.VMEM((2, 1, CROWS), f32),
+            pltpu.VMEM((2, 1, CROWS), f32),
+            pltpu.VMEM((2, HEAD, CROWS), f32),
+            pltpu.VMEM((2, 1, CROWS), f32),
             dma((72,)),
             dma((72,)),
             dma((CHUNKS, 40)),
             dma((CHUNKS, 40)),
-            dma((40,)),
-            dma((40,)),
+            dma((48,)),
+            dma((48,)),
+            dma((3,)),
         ],
         compiler_params=pltpu.CompilerParams(
             collective_id=0, has_side_effects=True, vmem_limit_bytes=VMEM_CAP
@@ -618,7 +732,21 @@
         w_out,
         jnp.asarray(freq[None], f32),
     )
-    return mixed, peak[0, :1], stat
+    return pl.pallas_call(
+        finish_kernel,
+        out_shape=(
+            jax.ShapeDtypeStruct((2, TOK, HEAD), bf),
+            jax.ShapeDtypeStruct((1,), f32),
+            jax.ShapeDtypeStruct((2, 2, TOK), f32),
+        ),
+        in_specs=vmem(3),
+        out_specs=(
+            pl.BlockSpec(memory_space=pltpu.VMEM),
+            pl.BlockSpec(memory_space=pltpu.SMEM),
+            pl.BlockSpec(memory_space=pltpu.VMEM),
+        ),
+        name="finish",
+    )(mixed, peak, stat)
 
 
 def solution(mesh):

time: 169 us -> 141 us (0.83)
  Pallas kernels: 163 us -> 140 us
  local copies, waits for them, and re-layouts: 4.38 us -> 0 us
    pallas_call x1, Pallas kernels: 163 us -> 138 us  [shards(): pl.pallas_call(layer_kernel, out_shape=(jax.ShapeDtypeStruct((2, TOK, HEA...]
    unnamed x2 -> x0, local copies, waits for them, and re-layouts: 3.19 us -> none
    pallas_call x0 -> x1, Pallas kernels: none -> 1.89 us  [shards(): pl.pallas_call(finish_kernel, out_shape=(jax.ShapeDtypeStruct((2, TOK, HE...]
where the time goes in v3:
time: 141 us
  Pallas kernels  140 us (99%)
    pallas_call x1, Pallas kernels, shards(): pl.pallas_call(layer_kernel, out_shape=(jax.ShapeDtypeStruct((2, TOK, HEA...  138 us

profile of v3, /device:TPU:1, one launch (start us, length us, event | category | flops | bytes accessed | tf_op | source)
XLA Modules:
  0.0 140.6 jit_solution(15979895140193500347)
XLA Ops:
  0.6 137.9 %layer.1 = (bf16[2,1024,128]{2,1,0:T(8,128)(2,1)}, f32[8,128]{1,0:T(8,128)}, f32[2,2,1024]{2,1,0:T(2,128)}) custom-call(bf16[2,1024,128]{2,1,0:T(8,128)(2,1)} %tok_hbm.1, bf16[3,4096,128]{2,1,0:T(8,128)(2,1)} %bitcast.3, f32[1,128]{1,0:T(1,128)} %bitcast.4, f32[1,128]{1,0:T(1,128)} %bitcast.5, bf16[128,4096]{1,0:T(8,128)(2,1)} %w_out_hbm.1, ...), custom_call_target="tpu_custom_call" | custom-call | tf_op jit(solution)/shard_map/layer/pallas_call | solution.py:667
  138.6 1.9 %finish.1 = (bf16[2,1024,128]{2,1,0:T(8,128)(2,1)}, f32[1]{0:T(128)}, f32[2,2,1024]{2,1,0:T(2,128)}) custom-call(bf16[2,1024,128]{2,1,0:T(8,128)(2,1)} %get-tuple-element.6.mixed, f32[8,128]{1,0:T(8,128)} %get-tuple-element.7.peak, f32[2,2,1024]{2,1,0:T(2,128)} %get-tuple-element.8.stat), custom_call_target="tpu_custom_call" | custom-call | tf_op jit(solution)/shard_map/finish/pallas_call | solution.py:735

commit v4 on v3

v4 whole, which is shorter than its diff:
```python
import contextlib
import math

import jax
import jax.numpy as jnp
import numpy as np
from jax import lax
from jax.experimental import pallas as pl
from jax.experimental.pallas import tpu as pltpu
from jax.sharding import Mesh
from jax.sharding import PartitionSpec as P

EPS = 1e-06
ROPE_BASE = 500000.0
NEG = -1e30
MESH = pl.DeviceIdType.MESH
HEAD = 128
TOK = 1024
CHUNKS = 2
CROWS = TOK // CHUNKS
WIDTH = 4096
BK = 512
VMEM_CAP = 60 * 1024 * 1024
SCALE = HEAD ** (-0.5)
LOG2E = math.log2(math.e)
DIRS = (1, -1)
PART = {1: 0, -1: 1}
CQ, CV, CK = 0, HEAD, 2 * HEAD


def scope(name):
    return contextlib.nullcontext()


def here():
    xh, xl = lax.axis_index("xh"), lax.axis_index("xl")
    return xh * 2 + xl, xh, xl, lax.axis_index("co"), lax.axis_index("z"), lax.axis_index("y")


def seq_of(x):
    return 1 - ((x + 1) // 2) % 2


def half_of(x):
    return 1 - x % 2


def at_x(x, core=None):
    dev = {"xl": x % 2, "xh": x // 2}
    if core is not None:
        dev["co"] = core
    return dev


class Sender:
    def __init__(self, ssem, rsem, region):
        self.ssem, self.rsem, self.region = ssem, rsem, region
        self.groups, self.keys = {}, {}
        self.leaving, self.arriving = {}, {}

    def __call__(self, src, dst, dev, group, key):
        g = self.groups.setdefault(group, len(self.groups))
        k = self.keys.setdefault(key, len(self.keys))
        size = math.prod(src.shape) * jnp.dtype(src.dtype).itemsize
        self.leaving[group] = self.leaving.get(group, 0) + size
        self.arriving[key] = self.arriving.get(key, 0) + size
        pltpu.make_async_remote_copy(
            src_ref=src,
            dst_ref=dst,
            send_sem=self.ssem.at[g],
            recv_sem=self.rsem.at[k],
            device_id=dev,
            device_id_type=MESH,
        ).start()

    def wait(self, *key):
        ref = self.region(self.arriving.pop(key))
        pltpu.make_async_copy(ref, ref, self.rsem.at[self.keys[key]]).wait()

    def flush(self):
        assert not self.arriving, self.arriving
        for group, size in self.leaving.items():
            ref = self.region(size)
            pltpu.make_async_copy(ref, ref, self.ssem.at[self.groups[group]]).wait()


class Gather:
    def __init__(self, name, buf, send, z, y, use):
        self.name, self.buf, self.send, self.use = name, buf, send, use
        self.first, self.second = (z, y), (y, z)

    def place(self, h, f, s):
        return (f % 4, s % 4) if h == 0 else (s % 4, f % 4)

    def at(self, h, df, ds):
        return self.place(h, self.first[h] + df, self.second[h] + ds)

    def move(self, h, df, ds, part, along, d, *key):
        zz, yy = self.at(h, df, ds)
        ref = self.buf.at[h, zz, yy] if part is None else self.buf.at[h, zz, yy, part]
        name = (("z", "y"), ("y", "z"))[h][along]
        me = (self.first[h], self.second[h])[along]
        self.send(ref, ref, {name: (me + d + 4) % 4}, self.name, (self.name, h, *key))

    def wait(self, h, *key):
        self.send.wait(self.name, h, *key)

    def start(self, h, part=None):
        for d in DIRS:
            self.move(h, 0, 0, part, 0, d, "p1", d)
            self.move(h, 0, 0, part, 1, d, "p2", 0, d)

    def near(self, h, d):
        self.wait(h, "p1", d)
        self.move(h, 4 - d, 0, PART[d], 0, d, "p1f")
        for e in DIRS:
            self.move(h, 4 - d, 0, None, 1, e, "p2", -d, e)

    def use_near(self, h, d):
        self.use(h, *self.at(h, 4 - d, 0))

    def pass_on(self, h, j):
        for d in DIRS:
            self.wait(h, "p2", j, d)
            self.move(h, j + 4, 4 - d, PART[d], 1, d, "p2f", j)

    def use_passed(self, h, j):
        for d in DIRS:
            self.use(h, *self.at(h, j + 4, 4 - d))

    def opposite(self, h):
        self.wait(h, "p1f")
        for d in DIRS:
            self.move(h, 2, 0, None, 1, d, "p2", 2, d)

    def use_opposite(self, h):
        self.use(h, *self.at(h, 2, 0))

    def last(self, h, j):
        self.wait(h, "p2f", j)
        self.use(h, *self.at(h, j + 4, 2))


def layer_kernel(
    tok_hbm, w_hbm, q_gain, k_gain, w_out_hbm, freq,
    mixed, peak, stat_out,
    tok, w_own, w_out, buf, w_far, gains, gains_far, cosf, sinf, acc, acc_far, zb, yb, inv, inv_in,
    q_all, k_all, v_all, q_far, k_far, v_far,
    wz, w_cols, buf2, o_far, acc2, ob, tops,
    sc0, sc1, top_r, den_r, acc_r, pace, k_norm,
    ssem, rsem, ins,
):
    loads = [
        pltpu.make_async_copy(src, dst, ins.at[i])
        for i, (src, dst) in enumerate(((tok_hbm, tok), (w_hbm, w_own), (w_out_hbm, w_out)))
    ]
    for cp in loads:
        cp.start()
    x, xh, xl, co, z, y = here()
    right, left, pair, same = (x + 1) % 4, (x + 3) % 4, 3 - x, xh * 2 + (1 - xl)
    other = {"co": 1 - co}
    peers = (
        [other] + [at_x((x + i) % 4, cc) for i in (1, 2, 3) for cc in (co, 1 - co)]
        + [{"z": (z + i) % 4} for i in (1, 2, 3)]
        + [{"y": (y + i) % 4} for i in (1, 2, 3)]
    )
    with scope("greet"):
        barrier = pltpu.get_barrier_semaphore()
        for dev in peers:
            pl.semaphore_signal(barrier, inc=1, device_id=dev, device_id_type=MESH)
        pl.semaphore_wait(barrier, len(peers))

    def region(size):
        for n in (1, 2, 3):
            if size % (n * 4096) == 0 and size <= n * WIDTH * HEAD * 2:
                return w_far.at[0:n, 0 : size // (n * HEAD * 2)]
        rows, rest = divmod(size, 64 * HEAD * 2)
        assert rest == 0 and rows % 16 == 0 and rows <= CROWS // 2, size
        return buf.at[0, :, :, :, :, 0:rows]

    send = Sender(ssem, rsem, region)
    sub = CROWS // 2

    def eighth(xx, cc):
        return 4 * half_of(xx) + 2 * cc + seq_of(xx)

    mine, far_tile = eighth(x, co), eighth(pair, 1 - co)
    part_of_mine = pl.ds(pl.multiple_of(seq_of(x) * CROWS, CROWS), CROWS)

    def send_tokens(ch):
        for h in (0, 1):
            dst = buf.at[ch, h, z, y, xh]
            for part, dev in ((xh, right), (1 - xh, left)):
                src = tok.at[ch, pl.ds(pl.multiple_of(part * CROWS + h * sub, sub), sub)]
                send(src, dst, at_x(dev), "rows", ("tok", ch, h))

    loads[0].wait()
    send_tokens(0)
    gains[0:1, :] = q_gain[...]
    gains[1:2, :] = k_gain[...]
    loads[1].wait()

    def w_rows(xx):
        return pl.ds(pl.multiple_of(((xx % 2) * 2 + co) * 1024, 1024), 1024)

    def send_w(j):
        send(w_own.at[j, w_rows(x)], w_far.at[j, w_rows(x)], at_x(pair), "w", ("far_w", j))

    def relay_w(j):
        send.wait("far_w", j)
        ref = w_far.at[j, w_rows(pair)]
        send(ref, ref, at_x(same), "w", ("same_w", j))
        send(ref, ref, other, "w", ("relayed", j == 1))

    def relay_w2(j):
        send.wait("same_w", j)
        ref = w_far.at[j, w_rows(pair + 1)]
        send(ref, ref, other, "w", ("relayed", j == 1))

    send_w(0)
    send_w(2)
    send_tokens(1)
    send_w(1)
    send(gains, gains_far, at_x(pair), "small", ("gains",))

    def dots(target, w, ch, h, blocks, zero=False, kinds=(0, 2, 1), at=0):
        lhs, rhs = [], []
        for zz, yy in blocks:
            lhs += [buf[ch, h, zz, yy, 0], buf[ch, h, zz, yy, 1]]
            rows = pl.ds(pl.multiple_of((zz * 4 + yy) * 256, 256), 256)
            some = [w[j, rows, :] for j in kinds]
            rhs.append(some[0] if len(some) == 1 else jnp.concatenate(some, axis=-1))
        lhs = jnp.concatenate(lhs, axis=-1)
        rhs = rhs[0] if len(rhs) == 1 else jnp.concatenate(rhs, axis=0)
        out = jnp.dot(lhs, rhs, preferred_element_type=jnp.float32)
        place = (pl.ds(ch * CROWS + h * sub, sub), slice(at, at + HEAD * len(kinds)))
        target[place] = out if zero else target[place] + out

    def gather_of(ch):
        return Gather(
            ("tokens", ch), buf.at[ch], send, z, y, lambda h, zz, yy: dots(acc, w_own, ch, h, [(zz, yy)])
        )

    def own_dot(ch, h):
        dots(acc, w_own, ch, h, [(z, y)], True)

    def far_dots(ch, kinds, at, lines=(0, 1, 3, 2)):
        for i in lines:
            for h in (0, 1):
                blocks = [g[ch].at(h, f, i) for f in range(4)]
                dots(acc_far, w_far, ch, h, blocks, i == 0, kinds, at)

    def tables():
        def some(i, carry):
            rows = pl.ds(pl.multiple_of(i * 256, 256), 256)
            p = lax.broadcasted_iota(jnp.int32, (256, HEAD), 0) + (mine * CROWS + i * 256)
            lane = lax.broadcasted_iota(jnp.int32, (256, HEAD), 1)
            angle = p.astype(jnp.float32) * freq[...]
            cosf[rows, :] = jnp.cos(angle)
            sine = jnp.sin(angle)
            sinf[rows, :] = jnp.where(lane < HEAD // 2, -sine, sine)
            return carry

        lax.fori_loop(0, CROWS // 256, some, 0)

    def squares(ch):
        for j, c in ((0, CQ), (1, CK)):
            cols = pl.ds(c, HEAD)
            for i in range(2):
                rows = pl.ds(ch * CROWS + i * sub, sub)
                a, b = acc[rows, cols], acc_far[rows, cols]
                zb[ch, z, j : j + 1, i * sub : (i + 1) * sub] = jnp.sum(
                    (a * a + b * b).T, axis=0, keepdims=True
                )
        ref = zb.at[ch, z]
        for i in (1, 2, 3):
            send(ref, ref, {"z": (z + i) % 4}, "small", ("zsum", ch))

    def totals(ch):
        send.wait("zsum", ch)
        yb[ch, y] = (zb[ch, 0] + zb[ch, 1]) + (zb[ch, 2] + zb[ch, 3])
        ref = yb.at[ch, y]
        for i in (1, 2, 3):
            send(ref, ref, {"y": (y + i) % 4}, "small", ("ysum", ch))

    def turned(a, j, g, ch, i):
        rows = pl.ds(ch * CROWS + i * sub, sub)
        t = a[rows, CK : CK + HEAD] if j else a[rows, CQ : CQ + HEAD]
        t = t * g[j : j + 1, :]
        table = slice(i * sub, (i + 1) * sub)
        return (t * cosf[table, :] + pltpu.roll(t, HEAD // 2, 1) * sinf[table, :]).astype(
            jnp.bfloat16
        )

    def give(name, ch, far, all_):
        slot = all_.at[ch, mine]
        send(far.at[ch], slot, at_x(pair), name, ("pair", name, ch))
        send(slot, slot, at_x(same), name, ("same", name, ch))
        send(slot, slot, other, name, ("near", ch))

    def take_pair(name, ch):
        ref = (k_all if name == "k" else v_all).at[ch, eighth(pair, co)]
        send.wait("pair", name, ch)
        send(ref, ref, at_x(same), name, ("fwd", name, ch))
        send(ref, ref, other, name, ("near", ch))

    def take_same(name, ch):
        ref = (k_all if name == "k" else v_all).at[ch, eighth(same, co)]
        send.wait("same", name, ch)
        send(ref, ref, other, name, ("near", ch))

    def take_fwd(name, ch):
        ref = (k_all if name == "k" else v_all).at[ch, eighth((x + 2) % 4, co)]
        send.wait("fwd", name, ch)
        send(ref, ref, other, name, ("near", ch))

    def values(ch):
        for i in range(2):
            here_rows = slice(i * sub, (i + 1) * sub)
            rows = pl.ds(ch * CROWS + i * sub, sub)
            v_far[ch, :, here_rows] = acc_far[rows, CV : CV + HEAD].T.astype(jnp.bfloat16)
            v_all[ch, mine, :, here_rows] = acc[rows, CV : CV + HEAD].T.astype(jnp.bfloat16)
        give("v", ch, v_far, v_all)

    def keys(ch):
        for i in range(2):
            here_rows = slice(i * sub, (i + 1) * sub)
            k_far[ch, here_rows, :] = turned(acc_far, 1, gains_far, ch, i)
            k_all[ch, mine, here_rows, :] = turned(acc, 1, gains, ch, i)
        give("k", ch, k_far, k_all)

    def queries(ch):
        for i in range(2):
            q_far[ch, i * sub : (i + 1) * sub, :] = turned(acc_far, 0, gains_far, ch, i)
        send(q_far.at[ch], q_all.at[ch, 1], at_x(pair, 1 - co), "rows", ("q", ch))
        for i in range(2):
            q_all[ch, 0, i * sub : (i + 1) * sub, :] = turned(acc, 0, gains, ch, i)

    def norms(ch):
        send.wait("ysum", ch)
        inv[ch, mine] = lax.rsqrt(
            ((yb[ch, 0] + yb[ch, 1]) + (yb[ch, 2] + yb[ch, 3])) / WIDTH + EPS
        )
        ref = inv.at[ch, mine]
        opposite = (x + 2) % 4
        for dev in (
            at_x(pair), at_x(pair, 1 - co), at_x(same), at_x(same, 1 - co),
            at_x(opposite), at_x(opposite, 1 - co), other,
        ):
            send(ref, ref, dev, "small", ("scale", ch))
        for dev in (right, left):
            send(ref, inv_in.at[ch, seq_of(x)], at_x(dev), "small", ("stats",))

    part = pl.ds(pl.multiple_of(co * 64, 64), 64)
    strip = pl.ds(pl.multiple_of((co * 2 + x % 2) * 32, 32), 32)

    def z_cols(zz):
        return pl.ds(pl.multiple_of((zz % 4) * 1024, 1024), 1024)

    def y_cols(yy):
        return pl.ds(pl.multiple_of((yy % 4) * 256, 256), 256)

    def cols_z():
        wz[z] = w_out[strip, z_cols(z)]
        for i in (1, 2, 3):
            send(
                w_out.at[strip, z_cols(z + i)], wz.at[z], {"z": (z + i) % 4}, "cols", ("wz",)
            )

    def cols_y():
        send.wait("wz")
        w_cols[:, y, xh, strip, :] = wz[:, :, y_cols(y)]
        for i in (1, 2, 3):
            send(
                wz.at[:, :, y_cols(y + i)],
                w_cols.at[:, y, xh, strip],
                {"y": (y + i) % 4},
                "cols",
                ("wy",),
            )

    def cols_same():
        send.wait("wy")
        ref = w_cols.at[:, :, xh, strip]
        send(ref, ref, at_x(same), "cols", ("ws",))

    def cols_x(i):
        ref = w_cols.at[2 * i : 2 * i + 2, :, xh, part]
        send(ref, ref, at_x(pair), "cols", ("wx", i))

    def cols_core(i):
        send.wait("wx", i)
        ref = w_cols.at[2 * i : 2 * i + 2, :, :, part]
        send(ref, ref, other, "core", ("wc",))

    best = []

    def columns(ch):
        def column(e, carry):
            for i in range(CROWS // HEAD):
                lanes = slice(i * HEAD, (i + 1) * HEAD)
                k_norm[e, lanes, :] = jnp.broadcast_to(inv[ch, e, 1:2, lanes], (HEAD, HEAD)).T
            return carry

        lax.fori_loop(0, 8, column, 0)

    def attend(ch):
        count = far_tile + 1
        total = count + mine + 1
        for i, e in enumerate((mine, far_tile)):
            pace[i] = inv[ch, e, 0:1, :] * (SCALE * LOG2E)

        top_r[...] = jnp.full((2, 1, CROWS), NEG, jnp.float32)
        den_r[...] = jnp.zeros((2, 1, CROWS), jnp.float32)
        acc_r[...] = jnp.zeros((2, HEAD, CROWS), jnp.float32)

        def where(t):
            own = (t + 16 - count) // 16
            return 1 - own, (1 - own) * (count - 1 - t) + own * (t - count)

        def score(t, into):
            which, j = where(t)
            raw = lax.dot_general(
                k_all[ch, j], q_all[ch, which], (((1,), (1,)), ((), ())),
                preferred_element_type=jnp.float32,
            )
            into[...] = raw * jnp.concatenate([k_norm[j]] * (CROWS // HEAD), axis=-1)

        def weigh(t, cur, masked):
            which, j = where(t)
            s = cur[...]
            if masked:
                r = lax.broadcasted_iota(jnp.int32, (BK, CROWS), 0)
                c = lax.broadcasted_iota(jnp.int32, (BK, CROWS), 1)
                s = jnp.where(r <= c, s, NEG)
            top, p = top_r[which], pace[which]
            new = jnp.maximum(top, jnp.max(s, axis=0, keepdims=True))
            e = jnp.exp2((s - new) * p)
            keep = jnp.exp2((top - new) * p)
            den_r[which] = den_r[which] * keep + jnp.sum(e, axis=0, keepdims=True)
            acc_r[which] = acc_r[which] * keep + jnp.dot(
                v_all[ch, j], e.astype(jnp.bfloat16), preferred_element_type=jnp.float32
            )
            top_r[which] = new

        score(0, sc0)
        score(1, sc1)
        weigh(0, sc0, True)

        def two(i, carry):
            t = 2 * i + 1
            score(t + 1, sc0)
            weigh(t, sc1, False)
            score(t + 2, sc1)
            weigh(t + 1, sc0, False)
            return carry

        lax.fori_loop(0, 3 + seq_of(x), two, 0)
        weigh(total - 1, sc1, True)
        for h in (0, 1):
            o_far[ch, h] = (
                (acc_r[1, :, h * sub : (h + 1) * sub] / den_r[1, :, h * sub : (h + 1) * sub])
                .T.astype(jnp.bfloat16)
            )
            dst = buf2.at[ch, h, z, y, xh]
            send(o_far.at[ch, h], dst, at_x(pair, 1 - co), "rows", ("back", ch, h))
        for h in (0, 1):
            buf2[ch, h, z, y, xh] = (
                (acc_r[0, :, h * sub : (h + 1) * sub] / den_r[0, :, h * sub : (h + 1) * sub])
                .T.astype(jnp.bfloat16)
            )
            g2[ch].start(h, xh)
        peaks_here = [jnp.max(top_r[i] * pace[i], axis=1, keepdims=True) for i in (0, 1)]
        best.append(jnp.maximum(*peaks_here) * (1 / LOG2E))

    def start_far(ch):
        for h in (0, 1):
            send.wait("back", ch, h)
            g2[ch].start(h, 1 - xh)

    def use2(ch, h, zz, yy, zero=False):
        lhs = jnp.concatenate([buf2[ch, h, zz, yy, 0], buf2[ch, h, zz, yy, 1]], axis=-1)
        rhs = jnp.concatenate([w_cols[zz, yy, 0], w_cols[zz, yy, 1]], axis=0)
        out = jnp.dot(lhs, rhs, preferred_element_type=jnp.float32)
        rows = pl.ds(ch * CROWS + h * sub, sub)
        acc2[rows, :] = out if zero else acc2[rows, :] + out

    g = [gather_of(0), gather_of(1)]
    g2 = [
        Gather(
            ("attended", ch),
            buf2.at[ch],
            send,
            z,
            y,
            lambda h, zz, yy, ch=ch: use2(ch, h, zz, yy),
        )
        for ch in (0, 1)
    ]

    def finish(ch, h):
        rows = pl.ds(ch * CROWS + h * sub, sub)
        to = pl.ds(pl.multiple_of(seq_of(x) * CROWS + h * sub, sub), sub)
        for i in (0, 1):
            ob[i, rows, :] = acc2[rows, i * HEAD : (i + 1) * HEAD].astype(jnp.bfloat16)
        for dev in (right, left):
            send(ob.at[dev // 2, rows], mixed.at[ch, to], at_x(dev), "rows", ("fin",))

    def begin(ch):
        for h in (0, 1):
            send.wait("tok", ch, h)
            g[ch].start(h)

    def both(method, *args):
        for h in (0, 1):
            method(h, *args)

    def nears(ga):
        for d in DIRS:
            both(ga.near, d)

    def use_nears(ga):
        for d in DIRS:
            both(ga.use_near, d)

    def own_take(ch):
        send.wait("scale", ch)
        columns(ch)
        send.wait("near", ch)
        send.wait("q", ch)

    with scope("begin0"):
        loads[2].wait()
        cols_z()
        begin(0)
    with scope("tables"):
        tables()
    with scope("middle0"):
        for h in (0, 1):
            own_dot(0, h)
        nears(g[0])
        use_nears(g[0])
        both(g[0].pass_on, 0)
        both(g[0].opposite)
        relay_w(0)
        both(g[0].use_passed, 0)
        both(g[0].use_opposite)
        both(g[0].pass_on, -1)
        both(g[0].use_passed, -1)
        both(g[0].pass_on, 1)
        relay_w(2)
    with scope("begin1"):
        begin(1)
    with scope("pass0"):
        both(g[0].pass_on, 2)
        both(g[0].use_passed, 1)
        relay_w2(0)
        relay_w(1)
        both(g[0].use_passed, 2)
    with scope("drain0a"):
        both(g[0].last, 0)
    with scope("near1"):
        nears(g[1])
    with scope("relay_w2"):
        relay_w2(2)
    with scope("drain0b"):
        both(g[0].last, -1)
        both(g[0].last, 1)
    with scope("pass1_0"):
        both(g[1].pass_on, 0)
    with scope("drain0c"):
        both(g[0].last, 2)
    with scope("have_w"):
        send.wait("relayed", False)
    with scope("far_qv0"):
        far_dots(0, (0, 2), 0)
        values(0)
    with scope("opp1"):
        both(g[1].opposite)
        relay_w2(1)
    with scope("uses1"):
        for h in (0, 1):
            own_dot(1, h)
        use_nears(g[1])
    with scope("have_wk"):
        send.wait("relayed", True)
        send.wait("gains")
    with scope("far_k0"):
        far_dots(0, (1,), CK)
        keys(0)
        queries(0)
        squares(0)
    with scope("take_v"):
        take_pair("v", 0)
        take_same("v", 0)
    with scope("pass1_m"):
        both(g[1].pass_on, -1)
    with scope("take_k"):
        take_pair("k", 0)
        take_same("k", 0)
    with scope("uses1b"):
        both(g[1].use_passed, 0)
        both(g[1].use_opposite)
        both(g[1].use_passed, -1)
    with scope("tot0"):
        totals(0)
    with scope("pass1_1"):
        both(g[1].pass_on, 1)
    with scope("take_f"):
        take_fwd("v", 0)
        norms(0)
    with scope("pass1_2"):
        both(g[1].pass_on, 2)
        cols_y()
    with scope("take_fk"):
        take_fwd("k", 0)
    with scope("uses1c"):
        both(g[1].use_passed, 1)
        both(g[1].use_passed, 2)
        far_dots(1, (0, 2), 0, (0, 1, 3))
        far_dots(1, (1,), CK, (0, 1, 3))
    with scope("take0"):
        own_take(0)
    with scope("attend0"):
        attend(0)
    with scope("drain1"):
        for j in (0, -1, 1, 2):
            both(g[1].last, j)
        far_dots(1, (0, 2), 0, (2,))
        values(1)
        far_dots(1, (1,), CK, (2,))
        keys(1)
        queries(1)
        squares(1)
    with scope("start_far0"):
        start_far(0)
    with scope("take_v1"):
        take_pair("v", 1)
        take_same("v", 1)
    with scope("tot1"):
        totals(1)
    with scope("near2"):
        nears(g2[0])
    with scope("take_k1"):
        take_pair("k", 1)
        take_same("k", 1)
        cols_same()
    with scope("norms1"):
        norms(1)
    with scope("pass2_0"):
        both(g2[0].pass_on, 0)
        both(g2[0].opposite)
    with scope("take_fv1"):
        take_fwd("v", 1)
    with scope("pass2_m"):
        both(g2[0].pass_on, -1)
    with scope("take_fk1"):
        take_fwd("k", 1)
    with scope("pass2_1"):
        both(g2[0].pass_on, 1)
    with scope("take1"):
        own_take(1)
    with scope("attend1"):
        attend(1)
    with scope("pass2_2"):
        send.wait("ws")
        cols_x(0)
        cols_x(1)
        both(g2[0].pass_on, 2)
    with scope("start_far1"):
        start_far(1)
        place = xl * 2 + co
        tops[place] = jnp.broadcast_to(jnp.maximum(*best), (8, HEAD))
        for dev in (other, at_x(same), at_x(same, 1 - co)):
            send(tops.at[place], tops.at[place], dev, "small", ("peak",))
    with scope("near3"):
        nears(g2[1])
        cols_core(0)
    with scope("pass3_0"):
        both(g2[1].pass_on, 0)
        both(g2[1].opposite)
    with scope("cols_core"):
        cols_core(1)
        send.wait("wc")
    with scope("use2"):
        for ch in (0, 1):
            for h in (0, 1):
                use2(ch, h, z, y, True)
        use_nears(g2[0])
        both(g2[0].use_passed, 0)
        both(g2[0].use_opposite)
        for j in (-1, 1, 2):
            both(g2[0].use_passed, j)
    with scope("drain2_0"):
        both(g2[1].pass_on, -1)
        for j in (0, -1, 1):
            both(g2[0].last, j)
        for h in (0, 1):
            g2[0].last(h, 2)
            finish(0, h)
    with scope("pass3"):
        both(g2[1].pass_on, 1)
        use_nears(g2[1])
        both(g2[1].use_passed, 0)
        both(g2[1].use_opposite)
        both(g2[1].use_passed, -1)
        both(g2[1].use_passed, 1)
        both(g2[1].pass_on, 2)
        both(g2[1].use_passed, 2)
    with scope("drain2_1"):
        for j in (0, -1, 1):
            both(g2[1].last, j)
        for h in (0, 1):
            g2[1].last(h, 2)
            finish(1, h)
    with scope("final"):
        send.wait("peak")
        peak[...] = jnp.maximum(jnp.maximum(tops[0], tops[1]), jnp.maximum(tops[2], tops[3]))
        send.wait("stats")
        for s in (0, 1):
            for i in (0, 1):
                stat_out[:, s, i * CROWS : (i + 1) * CROWS] = inv_in[s, i]
        send.wait("fin")
    with scope("wait_send"):
        send.flush()


def finish_kernel(mixed, peak, stat, mixed_out, peak_out, stat_out):
    mixed_out[...] = mixed[...]
    peak_out[0] = peak[0, 0]
    stat_out[...] = stat[...]


def vmem(count):
    return [pl.BlockSpec(memory_space=pltpu.VMEM)] * count


def shards(tokens, w_qkv, q_gain, k_gain, w_out):
    bf, f32 = jnp.bfloat16, jnp.float32
    dma = pltpu.SemaphoreType.DMA
    sub = CROWS // 2
    freq = ROPE_BASE ** (-(np.arange(HEAD) % (HEAD // 2) * 2.0) / HEAD)
    mixed, peak, stat = pl.pallas_call(
        layer_kernel,
        out_shape=(
            jax.ShapeDtypeStruct((2, TOK, HEAD), bf),
            jax.ShapeDtypeStruct((8, HEAD), f32),
            jax.ShapeDtypeStruct((2, 2, TOK), f32),
        ),
        in_specs=[
            pl.BlockSpec(memory_space=pltpu.VMEM if small else pl.ANY)
            for small in (False, False, True, True, False, True)
        ],
        out_specs=tuple(vmem(3)),
        scratch_shapes=[
            pltpu.VMEM((2, TOK, HEAD), bf),
            pltpu.VMEM((3, WIDTH, HEAD), bf),
            pltpu.VMEM((HEAD, WIDTH), bf),
            pltpu.VMEM((CHUNKS, 2, 4, 4, 2, sub, HEAD), bf),
            pltpu.VMEM((3, WIDTH, HEAD), bf),
            pltpu.VMEM((8, HEAD), f32),
            pltpu.VMEM((8, HEAD), f32),
            pltpu.VMEM((CROWS, HEAD), f32),
            pltpu.VMEM((CROWS, HEAD), f32),
            pltpu.VMEM((TOK, 3 * HEAD), f32),
            pltpu.VMEM((TOK, 3 * HEAD), f32),
            pltpu.VMEM((CHUNKS, 4, 2, CROWS), f32),
            pltpu.VMEM((CHUNKS, 4, 2, CROWS), f32),
            pltpu.VMEM((CHUNKS, 8, 2, CROWS), f32),
            pltpu.VMEM((CHUNKS, 2, 2, CROWS), f32),
            pltpu.VMEM((CHUNKS, 2, CROWS, HEAD), bf),
            pltpu.VMEM((CHUNKS, 8, CROWS, HEAD), bf),
            pltpu.VMEM((CHUNKS, 8, HEAD, CROWS), bf),
            pltpu.VMEM((CHUNKS, CROWS, HEAD), bf),
            pltpu.VMEM((CHUNKS, CROWS, HEAD), bf),
            pltpu.VMEM((CHUNKS, HEAD, CROWS), bf),
            pltpu.VMEM((4, 32, 1024), bf),
            pltpu.VMEM((4, 4, 2, HEAD, 256), bf),
            pltpu.VMEM((CHUNKS, 2, 4, 4, 2, sub, HEAD), bf),
            pltpu.VMEM((CHUNKS, 2, sub, HEAD), bf),
            pltpu.VMEM((TOK, 256), f32),
            pltpu.VMEM((2, TOK, HEAD), bf),
            pltpu.VMEM((4, 8, HEAD), f32),
            pltpu.VMEM((BK, CROWS), f32),
            pltpu.VMEM((BK, CROWS), f32),
            pltpu.VMEM((2, 1, CROWS), f32),
            pltpu.VMEM((2, 1, CROWS), f32),
            pltpu.VMEM((2, HEAD, CROWS), f32),
            pltpu.VMEM((2, 1, CROWS), f32),
            pltpu.VMEM((8, CROWS, HEAD), f32),
            dma((11,)),
            dma((169,)),
            dma((3,)),
        ],
        compiler_params=pltpu.CompilerParams(
            collective_id=0, has_side_effects=True, vmem_limit_bytes=VMEM_CAP
        ),
        name="layer",
    )(
        tokens,
        w_qkv.transpose(1, 0, 2),
        q_gain[None],
        k_gain[None],
        w_out,
        jnp.asarray(freq[None], f32),
    )
    return pl.pallas_call(
        finish_kernel,
        out_shape=(
            jax.ShapeDtypeStruct((2, TOK, HEAD), bf),
            jax.ShapeDtypeStruct((1,), f32),
            jax.ShapeDtypeStruct((2, 2, TOK), f32),
        ),
        in_specs=vmem(3),
        out_specs=(
            pl.BlockSpec(memory_space=pltpu.VMEM),
            pl.BlockSpec(memory_space=pltpu.SMEM),
            pl.BlockSpec(memory_space=pltpu.VMEM),
        ),
        name="finish",
    )(mixed, peak, stat)


def solution(mesh):
    finer = Mesh(mesh.devices.reshape(2, 2, 4, 4, 2), ("xl", "co", "z", "y", "xh"))
    tensor = ("z", "y", "xh")
    seq = ("xl", "co")
    placed = (P(None, seq, tensor), P(None, None, tensor), P(tensor), P(tensor), P(tensor, None))
    return jax.shard_map(
        shards,
        mesh=finer,
        in_specs=placed,
        out_specs=(P(None, seq, tensor), P(tensor), P(None, None, seq)),
        check_vma=False,
    )
```

time: 141 us -> 135 us (0.957)
  Pallas kernels: 140 us -> 134 us
    pallas_call x1, Pallas kernels: 138 us -> 132 us  [shards(): pl.pallas_call(layer_kernel, out_shape=(jax.ShapeDtypeStruct((2, TOK, HEA...]
where the time goes in v4:
time: 135 us
  Pallas kernels  134 us (99%)
    pallas_call x1, Pallas kernels, shards(): pl.pallas_call(layer_kernel, out_shape=(jax.ShapeDtypeStruct((2, TOK, HEA...  132 us

profile of v4, /device:TPU:1, one launch (start us, length us, event | category | flops | bytes accessed | tf_op | source)
XLA Modules:
  0.0 135.0 jit_solution(5559494809411733585)
XLA Ops:
  0.6 132.3 %layer.1 = (bf16[2,1024,128]{2,1,0:T(8,128)(2,1)}, f32[8,128]{1,0:T(8,128)}, f32[2,2,1024]{2,1,0:T(2,128)}) custom-call(bf16[2,1024,128]{2,1,0:T(8,128)(2,1)} %tok_hbm.1, bf16[3,4096,128]{2,1,0:T(8,128)(2,1)} %bitcast.3, f32[1,128]{1,0:T(1,128)} %bitcast.4, f32[1,128]{1,0:T(1,128)} %bitcast.5, bf16[128,4096]{1,0:T(8,128)(2,1)} %w_out_hbm.1, ...), custom_call_target="tpu_custom_call" | custom-call | tf_op jit(solution)/shard_map/layer/pallas_call | solution.py:743
  133.0 1.9 %finish.1 = (bf16[2,1024,128]{2,1,0:T(8,128)(2,1)}, f32[1]{0:T(128)}, f32[2,2,1024]{2,1,0:T(2,128)}) custom-call(bf16[2,1024,128]{2,1,0:T(8,128)(2,1)} %get-tuple-element.6.mixed, f32[8,128]{1,0:T(8,128)} %get-tuple-element.7.peak, f32[2,2,1024]{2,1,0:T(2,128)} %get-tuple-element.8.stat), custom_call_target="tpu_custom_call" | custom-call | tf_op jit(solution)/shard_map/finish/pallas_call | solution.py:807

commit v5 on v4

--- a/solution.py
+++ b/solution.py
@@ -25,7 +25,7 @@
 LOG2E = math.log2(math.e)
 DIRS = (1, -1)
 PART = {1: 0, -1: 1}
-CQ, CV, CK = 0, HEAD, 2 * HEAD
+CQ, CK, CV = 0, HEAD, 2 * HEAD
 
 
 def scope(name):
@@ -147,7 +147,7 @@
     tok, w_own, w_out, buf, w_far, gains, gains_far, cosf, sinf, acc, acc_far, zb, yb, inv, inv_in,
     q_all, k_all, v_all, q_far, k_far, v_far,
     wz, w_cols, buf2, o_far, acc2, ob, tops,
-    sc0, sc1, top_r, den_r, acc_r, pace, k_norm,
+    sc0, sc1, top_r, den_r, acc_r,
     ssem, rsem, ins,
 ):
     loads = [
@@ -210,20 +210,20 @@
         send.wait("far_w", j)
         ref = w_far.at[j, w_rows(pair)]
         send(ref, ref, at_x(same), "w", ("same_w", j))
-        send(ref, ref, other, "w", ("relayed", j == 1))
+        send(ref, ref, other, "w", ("relayed", j == 2))
 
     def relay_w2(j):
         send.wait("same_w", j)
         ref = w_far.at[j, w_rows(pair + 1)]
-        send(ref, ref, other, "w", ("relayed", j == 1))
+        send(ref, ref, other, "w", ("relayed", j == 2))
 
     send_w(0)
+    send_w(1)
+    send_tokens(1)
     send_w(2)
-    send_tokens(1)
-    send_w(1)
     send(gains, gains_far, at_x(pair), "small", ("gains",))
 
-    def dots(target, w, ch, h, blocks, zero=False, kinds=(0, 2, 1), at=0):
+    def dots(target, w, ch, h, blocks, zero=False, kinds=(0, 1, 2), at=0):
         lhs, rhs = [], []
         for zz, yy in blocks:
             lhs += [buf[ch, h, zz, yy, 0], buf[ch, h, zz, yy, 1]]
@@ -285,9 +285,9 @@
 
     def turned(a, j, g, ch, i):
         rows = pl.ds(ch * CROWS + i * sub, sub)
-        t = a[rows, CK : CK + HEAD] if j else a[rows, CQ : CQ + HEAD]
-        t = t * g[j : j + 1, :]
         table = slice(i * sub, (i + 1) * sub)
+        col = jnp.broadcast_to(inv[ch, j : j + 1, table], (HEAD, sub)).T
+        t = a[rows, j * HEAD : (j + 1) * HEAD] * col * g[j : j + 1, :]
         return (t * cosf[table, :] + pltpu.roll(t, HEAD // 2, 1) * sinf[table, :]).astype(
             jnp.bfloat16
         )
@@ -338,18 +338,9 @@
 
     def norms(ch):
         send.wait("ysum", ch)
-        inv[ch, mine] = lax.rsqrt(
-            ((yb[ch, 0] + yb[ch, 1]) + (yb[ch, 2] + yb[ch, 3])) / WIDTH + EPS
-        )
-        ref = inv.at[ch, mine]
-        opposite = (x + 2) % 4
-        for dev in (
-            at_x(pair), at_x(pair, 1 - co), at_x(same), at_x(same, 1 - co),
-            at_x(opposite), at_x(opposite, 1 - co), other,
-        ):
-            send(ref, ref, dev, "small", ("scale", ch))
+        inv[ch] = lax.rsqrt(((yb[ch, 0] + yb[ch, 1]) + (yb[ch, 2] + yb[ch, 3])) / WIDTH + EPS)
         for dev in (right, left):
-            send(ref, inv_in.at[ch, seq_of(x)], at_x(dev), "small", ("stats",))
+            send(inv.at[ch], inv_in.at[ch, seq_of(x)], at_x(dev), "small", ("stats",))
 
     part = pl.ds(pl.multiple_of(co * 64, 64), 64)
     strip = pl.ds(pl.multiple_of((co * 2 + x % 2) * 32, 32), 32)
@@ -395,20 +386,9 @@
 
     best = []
 
-    def columns(ch):
-        def column(e, carry):
-            for i in range(CROWS // HEAD):
-                lanes = slice(i * HEAD, (i + 1) * HEAD)
-                k_norm[e, lanes, :] = jnp.broadcast_to(inv[ch, e, 1:2, lanes], (HEAD, HEAD)).T
-            return carry
-
-        lax.fori_loop(0, 8, column, 0)
-
     def attend(ch):
         count = far_tile + 1
         total = count + mine + 1
-        for i, e in enumerate((mine, far_tile)):
-            pace[i] = inv[ch, e, 0:1, :] * (SCALE * LOG2E)
 
         top_r[...] = jnp.full((2, 1, CROWS), NEG, jnp.float32)
         den_r[...] = jnp.zeros((2, 1, CROWS), jnp.float32)
@@ -424,7 +404,7 @@
                 k_all[ch, j], q_all[ch, which], (((1,), (1,)), ((), ())),
                 preferred_element_type=jnp.float32,
             )
-            into[...] = raw * jnp.concatenate([k_norm[j]] * (CROWS // HEAD), axis=-1)
+            into[...] = raw
 
         def weigh(t, cur, masked):
             which, j = where(t)
@@ -433,7 +413,7 @@
                 r = lax.broadcasted_iota(jnp.int32, (BK, CROWS), 0)
                 c = lax.broadcasted_iota(jnp.int32, (BK, CROWS), 1)
                 s = jnp.where(r <= c, s, NEG)
-            top, p = top_r[which], pace[which]
+            top, p = top_r[which], SCALE * LOG2E
             new = jnp.maximum(top, jnp.max(s, axis=0, keepdims=True))
             e = jnp.exp2((s - new) * p)
             keep = jnp.exp2((top - new) * p)
@@ -470,8 +450,8 @@
                 .T.astype(jnp.bfloat16)
             )
             g2[ch].start(h, xh)
-        peaks_here = [jnp.max(top_r[i] * pace[i], axis=1, keepdims=True) for i in (0, 1)]
-        best.append(jnp.maximum(*peaks_here) * (1 / LOG2E))
+        peaks_here = [jnp.max(top_r[i], axis=1, keepdims=True) for i in (0, 1)]
+        best.append(jnp.maximum(*peaks_here) * SCALE)
 
     def start_far(ch):
         for h in (0, 1):
@@ -524,8 +504,6 @@
             both(ga.use_near, d)
 
     def own_take(ch):
-        send.wait("scale", ch)
-        columns(ch)
         send.wait("near", ch)
         send.wait("q", ch)
 
@@ -548,21 +526,21 @@
         both(g[0].pass_on, -1)
         both(g[0].use_passed, -1)
         both(g[0].pass_on, 1)
-        relay_w(2)
+        relay_w(1)
     with scope("begin1"):
         begin(1)
     with scope("pass0"):
         both(g[0].pass_on, 2)
         both(g[0].use_passed, 1)
         relay_w2(0)
-        relay_w(1)
+        relay_w(2)
         both(g[0].use_passed, 2)
     with scope("drain0a"):
         both(g[0].last, 0)
     with scope("near1"):
         nears(g[1])
     with scope("relay_w2"):
-        relay_w2(2)
+        relay_w2(1)
     with scope("drain0b"):
         both(g[0].last, -1)
         both(g[0].last, 1)
@@ -572,86 +550,85 @@
         both(g[0].last, 2)
     with scope("have_w"):
         send.wait("relayed", False)
-    with scope("far_qv0"):
-        far_dots(0, (0, 2), 0)
-        values(0)
+    with scope("far_qk0"):
+        far_dots(0, (0, 1), CQ)
+        squares(0)
     with scope("opp1"):
         both(g[1].opposite)
-        relay_w2(1)
+        relay_w2(2)
     with scope("uses1"):
         for h in (0, 1):
             own_dot(1, h)
         use_nears(g[1])
-    with scope("have_wk"):
+        send.wait("gains")
+    with scope("tot0"):
+        totals(0)
+    with scope("have_wv"):
         send.wait("relayed", True)
-        send.wait("gains")
-    with scope("far_k0"):
-        far_dots(0, (1,), CK)
+    with scope("far_v0"):
+        far_dots(0, (2,), CV)
+        values(0)
+    with scope("norms0"):
+        norms(0)
         keys(0)
         queries(0)
-        squares(0)
+    with scope("pass1_m"):
+        both(g[1].pass_on, -1)
+        both(g[1].use_passed, 0)
+        both(g[1].use_opposite)
+        both(g[1].use_passed, -1)
     with scope("take_v"):
         take_pair("v", 0)
         take_same("v", 0)
-    with scope("pass1_m"):
-        both(g[1].pass_on, -1)
+    with scope("pass1_1"):
+        both(g[1].pass_on, 1)
     with scope("take_k"):
         take_pair("k", 0)
         take_same("k", 0)
-    with scope("uses1b"):
-        both(g[1].use_passed, 0)
-        both(g[1].use_opposite)
-        both(g[1].use_passed, -1)
-    with scope("tot0"):
-        totals(0)
-    with scope("pass1_1"):
-        both(g[1].pass_on, 1)
-    with scope("take_f"):
-        take_fwd("v", 0)
-        norms(0)
     with scope("pass1_2"):
         both(g[1].pass_on, 2)
         cols_y()
-    with scope("take_fk"):
-        take_fwd("k", 0)
     with scope("uses1c"):
         both(g[1].use_passed, 1)
         both(g[1].use_passed, 2)
-        far_dots(1, (0, 2), 0, (0, 1, 3))
-        far_dots(1, (1,), CK, (0, 1, 3))
+        far_dots(1, (0, 1), CQ, (0, 1, 3))
+    with scope("take_f"):
+        take_fwd("v", 0)
+        take_fwd("k", 0)
+    with scope("far_v1"):
+        far_dots(1, (2,), CV, (0, 1, 3))
+    with scope("drain1"):
+        for j in (0, -1, 1, 2):
+            both(g[1].last, j)
+    with scope("far1"):
+        far_dots(1, (0, 1), CQ, (2,))
+        squares(1)
+        far_dots(1, (2,), CV, (2,))
+        values(1)
     with scope("take0"):
         own_take(0)
     with scope("attend0"):
         attend(0)
-    with scope("drain1"):
-        for j in (0, -1, 1, 2):
-            both(g[1].last, j)
-        far_dots(1, (0, 2), 0, (2,))
-        values(1)
-        far_dots(1, (1,), CK, (2,))
+    with scope("tot1"):
+        totals(1)
+        take_pair("v", 1)
+        take_same("v", 1)
+    with scope("start_far0"):
+        start_far(0)
+    with scope("norms1"):
+        norms(1)
         keys(1)
         queries(1)
-        squares(1)
-    with scope("start_far0"):
-        start_far(0)
-    with scope("take_v1"):
-        take_pair("v", 1)
-        take_same("v", 1)
-    with scope("tot1"):
-        totals(1)
+        take_fwd("v", 1)
     with scope("near2"):
         nears(g2[0])
     with scope("take_k1"):
         take_pair("k", 1)
         take_same("k", 1)
         cols_same()
-    with scope("norms1"):
-        norms(1)
     with scope("pass2_0"):
         both(g2[0].pass_on, 0)
         both(g2[0].opposite)
-    with scope("take_fv1"):
-        take_fwd("v", 1)
     with scope("pass2_m"):
         both(g2[0].pass_on, -1)
     with scope("take_fk1"):
@@ -766,7 +743,7 @@
             pltpu.VMEM((TOK, 3 * HEAD), f32),
             pltpu.VMEM((CHUNKS, 4, 2, CROWS), f32),
             pltpu.VMEM((CHUNKS, 4, 2, CROWS), f32),
-            pltpu.VMEM((CHUNKS, 8, 2, CROWS), f32),
+            pltpu.VMEM((CHUNKS, 2, CROWS), f32),
             pltpu.VMEM((CHUNKS, 2, 2, CROWS), f32),
             pltpu.VMEM((CHUNKS, 2, CROWS, HEAD), bf),
             pltpu.VMEM((CHUNKS, 8, CROWS, HEAD), bf),
@@ -786,8 +763,6 @@
             pltpu.VMEM((2, 1, CROWS), f32),
             pltpu.VMEM((2, 1, CROWS), f32),
             pltpu.VMEM((2, HEAD, CROWS), f32),
-            pltpu.VMEM((2, 1, CROWS), f32),
-            pltpu.VMEM((8, CROWS, HEAD), f32),
             dma((11,)),
             dma((169,)),
             dma((3,)),

time: 135 us -> 130 us (0.963)
  Pallas kernels: 134 us -> 129 us
    pallas_call x1, Pallas kernels: 132 us -> 128 us  [shards(): pl.pallas_call(layer_kernel, out_shape=(jax.ShapeDtypeStruct((2, TOK, HEA...]
where the time goes in v5:
time: 130 us
  Pallas kernels  129 us (99%)
    pallas_call x1, Pallas kernels, shards(): pl.pallas_call(layer_kernel, out_shape=(jax.ShapeDtypeStruct((2, TOK, HEA...  128 us

profile of v5, /device:TPU:1, one launch (start us, length us, event | category | flops | bytes accessed | tf_op | source)
XLA Modules:
  0.0 130.2 jit_solution(10404904664666295590)
XLA Ops:
  0.6 127.5 %layer.1 = (bf16[2,1024,128]{2,1,0:T(8,128)(2,1)}, f32[8,128]{1,0:T(8,128)}, f32[2,2,1024]{2,1,0:T(2,128)}) custom-call(bf16[2,1024,128]{2,1,0:T(8,128)(2,1)} %tok_hbm.1, bf16[3,4096,128]{2,1,0:T(8,128)(2,1)} %bitcast.3, f32[1,128]{1,0:T(1,128)} %bitcast.4, f32[1,128]{1,0:T(1,128)} %bitcast.5, bf16[128,4096]{1,0:T(8,128)(2,1)} %w_out_hbm.1, ...), custom_call_target="tpu_custom_call" | custom-call | tf_op jit(solution)/shard_map/layer/pallas_call | solution.py:720
  128.2 1.9 %finish.1 = (bf16[2,1024,128]{2,1,0:T(8,128)(2,1)}, f32[1]{0:T(128)}, f32[2,2,1024]{2,1,0:T(2,128)}) custom-call(bf16[2,1024,128]{2,1,0:T(8,128)(2,1)} %get-tuple-element.6.mixed, f32[8,128]{1,0:T(8,128)} %get-tuple-element.7.peak, f32[2,2,1024]{2,1,0:T(2,128)} %get-tuple-element.8.stat), custom_call_target="tpu_custom_call" | custom-call | tf_op jit(solution)/shard_map/finish/pallas_call | solution.py:782

commit v6 on v5

--- a/solution.py
+++ b/solution.py
@@ -107,21 +107,25 @@
 
     def start(self, h, part=None):
         for d in DIRS:
-            self.move(h, 0, 0, part, 0, d, "p1", d)
-            self.move(h, 0, 0, part, 1, d, "p2", 0, d)
-
-    def near(self, h, d):
-        self.wait(h, "p1", d)
-        self.move(h, 4 - d, 0, PART[d], 0, d, "p1f")
-        for e in DIRS:
-            self.move(h, 4 - d, 0, None, 1, e, "p2", -d, e)
+            self.move(h, 0, 0, part, 0, d, "p1")
+            self.move(h, 0, 0, part, 1, d, "p2", 0)
+
+    def near(self, h):
+        self.wait(h, "p1")
+        for d in DIRS:
+            self.move(h, 4 - d, 0, PART[d], 0, d, "p1f")
+
+    def spread(self, h):
+        for d in DIRS:
+            for e in DIRS:
+                self.move(h, 4 - d, 0, None, 1, e, "p2", -d)
 
     def use_near(self, h, d):
         self.use(h, *self.at(h, 4 - d, 0))
 
     def pass_on(self, h, j):
+        self.wait(h, "p2", j)
         for d in DIRS:
-            self.wait(h, "p2", j, d)
             self.move(h, j + 4, 4 - d, PART[d], 1, d, "p2f", j)
 
     def use_passed(self, h, j):
@@ -131,7 +135,7 @@
     def opposite(self, h):
         self.wait(h, "p1f")
         for d in DIRS:
-            self.move(h, 2, 0, None, 1, d, "p2", 2, d)
+            self.move(h, 2, 0, None, 1, d, "p2", 2)
 
     def use_opposite(self, h):
         self.use(h, *self.at(h, 2, 0))
@@ -142,9 +146,9 @@
 
 
 def layer_kernel(
-    tok_hbm, w_hbm, q_gain, k_gain, w_out_hbm, freq,
+    tok_hbm, w_hbm, q_gain, k_gain, w_out_hbm, freq_hbm,
     mixed, peak, stat_out,
-    tok, w_own, w_out, buf, w_far, gains, gains_far, cosf, sinf, acc, acc_far, zb, yb, inv, inv_in,
+    tok, w_own, w_out, freq, buf, w_far, gains, gains_far, cosf, sinf, acc, acc_far, zb, yb, inv, inv_in,
     q_all, k_all, v_all, q_far, k_far, v_far,
     wz, w_cols, buf2, o_far, acc2, ob, tops,
     sc0, sc1, top_r, den_r, acc_r,
@@ -152,7 +156,12 @@
 ):
     loads = [
         pltpu.make_async_copy(src, dst, ins.at[i])
-        for i, (src, dst) in enumerate(((tok_hbm, tok), (w_hbm, w_own), (w_out_hbm, w_out)))
+        for i, (src, dst) in enumerate(
+            (
+                (tok_hbm, tok), (w_hbm, w_own), (w_out_hbm, w_out), (freq_hbm, freq),
+                (q_gain, gains.at[0:1]), (k_gain, gains.at[1:2]),
+            )
+        )
     ]
     for cp in loads:
         cp.start()
@@ -196,9 +205,9 @@
 
     loads[0].wait()
     send_tokens(0)
-    gains[0:1, :] = q_gain[...]
-    gains[1:2, :] = k_gain[...]
     loads[1].wait()
+    for cp in loads[3:]:
+        cp.wait()
 
     def w_rows(xx):
         return pl.ds(pl.multiple_of(((xx % 2) * 2 + co) * 1024, 1024), 1024)
@@ -496,8 +505,8 @@
             method(h, *args)
 
     def nears(ga):
-        for d in DIRS:
-            both(ga.near, d)
+        both(ga.near)
+        both(ga.spread)
 
     def use_nears(ga):
         for d in DIRS:
@@ -595,37 +604,39 @@
     with scope("take_f"):
         take_fwd("v", 0)
         take_fwd("k", 0)
-    with scope("far_v1"):
-        far_dots(1, (2,), CV, (0, 1, 3))
     with scope("drain1"):
         for j in (0, -1, 1, 2):
             both(g[1].last, j)
     with scope("far1"):
         far_dots(1, (0, 1), CQ, (2,))
         squares(1)
-        far_dots(1, (2,), CV, (2,))
-        values(1)
+        cols_same()
     with scope("take0"):
         own_take(0)
     with scope("attend0"):
         attend(0)
+    with scope("far_v1"):
+        far_dots(1, (2,), CV)
+        values(1)
     with scope("tot1"):
         totals(1)
-        take_pair("v", 1)
-        take_same("v", 1)
     with scope("start_far0"):
         start_far(0)
     with scope("norms1"):
         norms(1)
         keys(1)
         queries(1)
-        take_fwd("v", 1)
+    with scope("take_v1"):
+        take_pair("v", 1)
+        take_same("v", 1)
     with scope("near2"):
         nears(g2[0])
     with scope("take_k1"):
         take_pair("k", 1)
         take_same("k", 1)
-        cols_same()
+        take_fwd("v", 1)
+        send.wait("ws")
+        cols_x(0)
     with scope("pass2_0"):
         both(g2[0].pass_on, 0)
         both(g2[0].opposite)
@@ -640,8 +651,6 @@
     with scope("attend1"):
         attend(1)
     with scope("pass2_2"):
-        send.wait("ws")
-        cols_x(0)
         cols_x(1)
         both(g2[0].pass_on, 2)
     with scope("start_far1"):
@@ -651,13 +660,15 @@
         for dev in (other, at_x(same), at_x(same, 1 - co)):
             send(tops.at[place], tops.at[place], dev, "small", ("peak",))
     with scope("near3"):
+        cols_core(0)
         nears(g2[1])
-        cols_core(0)
     with scope("pass3_0"):
         both(g2[1].pass_on, 0)
         both(g2[1].opposite)
+    with scope("pass3_m"):
+        cols_core(1)
+        both(g2[1].pass_on, -1)
     with scope("cols_core"):
-        cols_core(1)
         send.wait("wc")
     with scope("use2"):
         for ch in (0, 1):
@@ -668,15 +679,15 @@
         both(g2[0].use_opposite)
         for j in (-1, 1, 2):
             both(g2[0].use_passed, j)
+    with scope("pass3_1"):
+        both(g2[1].pass_on, 1)
     with scope("drain2_0"):
-        both(g2[1].pass_on, -1)
         for j in (0, -1, 1):
             both(g2[0].last, j)
         for h in (0, 1):
             g2[0].last(h, 2)
             finish(0, h)
     with scope("pass3"):
-        both(g2[1].pass_on, 1)
         use_nears(g2[1])
         both(g2[1].use_passed, 0)
         both(g2[1].use_opposite)
@@ -724,15 +735,13 @@
             jax.ShapeDtypeStruct((8, HEAD), f32),
             jax.ShapeDtypeStruct((2, 2, TOK), f32),
         ),
-        in_specs=[
-            pl.BlockSpec(memory_space=pltpu.VMEM if small else pl.ANY)
-            for small in (False, False, True, True, False, True)
-        ],
+        in_specs=[pl.BlockSpec(memory_space=pltpu.HBM)] * 6,
         out_specs=tuple(vmem(3)),
         scratch_shapes=[
             pltpu.VMEM((2, TOK, HEAD), bf),
             pltpu.VMEM((3, WIDTH, HEAD), bf),
             pltpu.VMEM((HEAD, WIDTH), bf),
+            pltpu.VMEM((1, HEAD), f32),
             pltpu.VMEM((CHUNKS, 2, 4, 4, 2, sub, HEAD), bf),
             pltpu.VMEM((3, WIDTH, HEAD), bf),
             pltpu.VMEM((8, HEAD), f32),
@@ -764,8 +773,8 @@
             pltpu.VMEM((2, 1, CROWS), f32),
             pltpu.VMEM((2, HEAD, CROWS), f32),
             dma((11,)),
-            dma((169,)),
-            dma((3,)),
+            dma((129,)),
+            dma((6,)),
         ],
         compiler_params=pltpu.CompilerParams(
             collective_id=0, has_side_effects=True, vmem_limit_bytes=VMEM_CAP

time: 130 us -> 128 us (0.985); the launches traced: 130 us -> 126 us
  Pallas kernels: 129 us -> 125 us
    pallas_call x1, Pallas kernels: 128 us -> 123 us  [shards(): pl.pallas_call(layer_kernel, out_shape=(jax.ShapeDtypeStruct((2, TOK, HEA...]
where the time goes in v6:
time: 128 us; the launch traced here: 126 us
  Pallas kernels  125 us (98%)
    pallas_call x1, Pallas kernels, shards(): pl.pallas_call(layer_kernel, out_shape=(jax.ShapeDtypeStruct((2, TOK, HEA...  123 us

profile of v6, /device:TPU:1, one launch (start us, length us, event | category | flops | bytes accessed | tf_op | source)
XLA Modules:
  0.0 125.9 jit_solution(11952545076848125667)
XLA Ops:
  0.6 123.2 %layer.1 = (bf16[2,1024,128]{2,1,0:T(8,128)(2,1)}, f32[8,128]{1,0:T(8,128)}, f32[2,2,1024]{2,1,0:T(2,128)}) custom-call(bf16[2,1024,128]{2,1,0:T(8,128)(2,1)} %tok_hbm.1, bf16[3,4096,128]{2,1,0:T(8,128)(2,1)} %bitcast.3, f32[1,128]{1,0:T(1,128)} %bitcast.4, f32[1,128]{1,0:T(1,128)} %bitcast.5, bf16[128,4096]{1,0:T(8,128)(2,1)} %w_out_hbm.1, ...), custom_call_target="tpu_custom_call" | custom-call | tf_op jit(solution)/shard_map/layer/pallas_call | solution.py:731
  123.9 1.9 %finish.1 = (bf16[2,1024,128]{2,1,0:T(8,128)(2,1)}, f32[1]{0:T(128)}, f32[2,2,1024]{2,1,0:T(2,128)}) custom-call(bf16[2,1024,128]{2,1,0:T(8,128)(2,1)} %get-tuple-element.6.mixed, f32[8,128]{1,0:T(8,128)} %get-tuple-element.7.peak, f32[2,2,1024]{2,1,0:T(2,128)} %get-tuple-element.8.stat), custom_call_target="tpu_custom_call" | custom-call | tf_op jit(solution)/shard_map/finish/pallas_call | solution.py:791

commit v7 on v6

--- a/solution.py
+++ b/solution.py
@@ -100,10 +100,11 @@
         ref = self.buf.at[h, zz, yy] if part is None else self.buf.at[h, zz, yy, part]
         name = (("z", "y"), ("y", "z"))[h][along]
         me = (self.first[h], self.second[h])[along]
-        self.send(ref, ref, {name: (me + d + 4) % 4}, self.name, (self.name, h, *key))
+        self.send(ref, ref, {name: (me + d + 4) % 4}, self.name, (self.name, *key))
 
     def wait(self, h, *key):
-        self.send.wait(self.name, h, *key)
+        if h == 0:
+            self.send.wait(self.name, *key)
 
     def start(self, h, part=None):
         for d in DIRS:
@@ -773,7 +774,7 @@
             pltpu.VMEM((2, 1, CROWS), f32),
             pltpu.VMEM((2, HEAD, CROWS), f32),
             dma((11,)),
-            dma((129,)),
+            dma((89,)),
             dma((6,)),
         ],
         compiler_params=pltpu.CompilerParams(

time: 128 us -> 128 us (level); the launches traced: 126 us -> 127 us
  Pallas kernels: 125 us -> 127 us
    pallas_call x1, Pallas kernels: 123 us -> 125 us  [shards(): pl.pallas_call(layer_kernel, out_shape=(jax.ShapeDtypeStruct((2, TOK, HEA...]
where the time goes in v7:
time: 128 us; the launch traced here: 127 us
  Pallas kernels  127 us (99%)
    pallas_call x1, Pallas kernels, shards(): pl.pallas_call(layer_kernel, out_shape=(jax.ShapeDtypeStruct((2, TOK, HEA...  125 us

profile of v7, /device:TPU:1, one launch (start us, length us, event | category | flops | bytes accessed | tf_op | source)
XLA Modules:
  0.0 127.4 jit_solution(14393967973415781112)
XLA Ops:
  0.6 124.7 %layer.1 = (bf16[2,1024,128]{2,1,0:T(8,128)(2,1)}, f32[8,128]{1,0:T(8,128)}, f32[2,2,1024]{2,1,0:T(2,128)}) custom-call(bf16[2,1024,128]{2,1,0:T(8,128)(2,1)} %tok_hbm.1, bf16[3,4096,128]{2,1,0:T(8,128)(2,1)} %bitcast.3, f32[1,128]{1,0:T(1,128)} %bitcast.4, f32[1,128]{1,0:T(1,128)} %bitcast.5, bf16[128,4096]{1,0:T(8,128)(2,1)} %w_out_hbm.1, ...), custom_call_target="tpu_custom_call" | custom-call | tf_op jit(solution)/shard_map/layer/pallas_call | solution.py:732
  125.4 1.9 %finish.1 = (bf16[2,1024,128]{2,1,0:T(8,128)(2,1)}, f32[1]{0:T(128)}, f32[2,2,1024]{2,1,0:T(2,128)}) custom-call(bf16[2,1024,128]{2,1,0:T(8,128)(2,1)} %get-tuple-element.6.mixed, f32[8,128]{1,0:T(8,128)} %get-tuple-element.7.peak, f32[2,2,1024]{2,1,0:T(2,128)} %get-tuple-element.8.stat), custom_call_target="tpu_custom_call" | custom-call | tf_op jit(solution)/shard_map/finish/pallas_call | solution.py:792
